TPU v7x, 8 devices: a whole 2x2x1 slice. The times are simulated.
8 devices in a mesh: data: 1 (over z), pp: 2 (over y), ep: 4 (over x, core).
Axes of the slice: x: 2, y: 2, z: 1, core: 2. Of those that a mesh axis runs over, the one named last changes fastest.
Arguments:
- expert_out: bfloat16 [2, 1, 128, 256, 4096], P(('data', 'pp'), None, 'ep')
- expert_ids: int32 [2, 1, 4, 512, 8], P(('data', 'pp'), None, 'ep')
- slot_ids: int32 [2, 1, 4, 512, 8], P(('data', 'pp'), None, 'ep')
- gates: float32 [2, 1, 4, 512, 8], P(('data', 'pp'), None, 'ep')
- resid: bfloat16 [2, 1, 4, 512, 4096], P(('data', 'pp'), None, 'ep')
- norm_scale: float32 [2, 4096], P('pp')
- w_query: bfloat16 [2, 4096, 12288], P('pp')
- w_key: bfloat16 [2, 4096, 12288], P('pp')
- w_value: bfloat16 [2, 4096, 12288], P('pp')
- w_out: bfloat16 [2, 96, 128, 4096], P('pp')
Outputs:
- output: bfloat16 [2, 1, 4, 512, 4096], P(('data', 'pp'), None, 'ep')
All inputs are finite; a program needn't handle non-finite values.
Results may differ from a plain program's by a relative error of at most 0.0123938.
Values are sent between devices in bfloat16 or wider.
A program may use at most 2 GiB of HBM per device.

v0:
```python
import jax
import jax.numpy as jnp
from jax import lax
from jax.sharding import PartitionSpec as P

NORM_EPS = 1e-6


def take_rows(row_table, flat_ids):
    return jnp.take(row_table, flat_ids, axis=0, mode='clip')


def combine_rows(row_table, flat_ids, weights, resid):
    gathered = jax.vmap(take_rows)(row_table, flat_ids)
    mixed = jnp.sum(gathered.astype(jnp.float32) * weights[..., None], axis=3)
    return (resid.astype(jnp.float32) + mixed).astype(jnp.bfloat16)


def attend_block(arrived, gain_row, w_query, w_key, w_value, w_out):
    head_count, head_dim = w_out.shape[0], w_out.shape[1]
    seq_len = arrived.shape[2]
    x_float = arrived.astype(jnp.float32)
    inv_rms = lax.rsqrt(jnp.mean(jnp.square(x_float), axis=-1, keepdims=True) + NORM_EPS)
    normed = (x_float * inv_rms * gain_row).astype(jnp.bfloat16)
    head_shape = arrived.shape[:3] + (head_count, head_dim)

    def project(w_mat):
        return jnp.einsum('mbld,de->mble', normed, w_mat, preferred_element_type=jnp.float32).astype(jnp.bfloat16).reshape(head_shape)

    q_heads = project(w_query)
    k_heads = project(w_key)
    v_heads = project(w_value)
    scores = jnp.einsum('mbqhe,mbkhe->mbhqk', q_heads, k_heads, preferred_element_type=jnp.float32) * head_dim ** -0.5
    positions = jnp.arange(seq_len)
    causal = positions[:, None] >= positions[None, :]
    attn_prob = jax.nn.softmax(jnp.where(causal, scores, -jnp.inf), axis=-1).astype(jnp.bfloat16)
    context = jnp.einsum('mbhqk,mbkhe->mbqhe', attn_prob, v_heads, preferred_element_type=jnp.float32).astype(jnp.bfloat16)
    proj = jnp.einsum('mbqhe,hed->mbqd', context, w_out, preferred_element_type=jnp.float32).astype(jnp.bfloat16)
    return (x_float + proj.astype(jnp.float32)).astype(jnp.bfloat16)


def solution(mesh):
    stages = mesh.shape['pp']
    ep_size = mesh.shape['ep']
    shift_pairs = [(src, (src + 1) % stages) for src in range(stages)]
    token_spec = P(('data', 'pp'), None, 'ep', None, None)
    weight_spec = P('pp', None, None)

    def local_step(expert_out, expert_ids, slot_ids, gates, resid, norm_scale, w_query, w_key, w_value, w_out):
        own_out = expert_out[0]
        micro_count, local_experts, capacity, model_dim = own_out.shape
        slot_dev = capacity // ep_size
        split_view = own_out.reshape(micro_count, local_experts, ep_size, slot_dev, model_dim)
        received = lax.all_to_all(split_view, 'ep', 2, 1, tiled=True)
        row_table = received.reshape(micro_count, local_experts * ep_size * slot_dev, model_dim)
        own_slots = slot_ids[0]
        is_kept = own_slots >= 0
        slot_base = lax.axis_index('ep') * slot_dev
        flat_ids = expert_ids[0] * slot_dev + jnp.where(is_kept, own_slots - slot_base, 0)
        weights = jnp.where(is_kept, gates[0], 0.0)
        combined = combine_rows(row_table, flat_ids, weights, resid[0])
        arrived = lax.ppermute(combined, 'pp', shift_pairs)
        result = attend_block(arrived, norm_scale[0], w_query[0], w_key[0], w_value[0], w_out[0])
        return result[None]

    return jax.shard_map(local_step, mesh=mesh, in_specs=(token_spec, token_spec, token_spec, token_spec, token_spec, P('pp', None), weight_spec, weight_spec, weight_spec, P('pp', None, None, None)), out_specs=token_spec, check_vma=False)
```

profile of v0, /device:TPU:0, one launch (start us, length us, event | category | flops | bytes accessed | tf_op | source)
XLA Modules:
  0.0 1494.4 jit_solution(1502766319209189102)
XLA Ops:
  0.0 44.4 %copy.33 = bf16[1,32,4,64,4096]{4,3,1,0,2:T(8,128)(2,1)} copy(bf16[1,32,4,64,4096]{4,3,2,1,0:T(8,128)(2,1)} %bitcast.1) | data formatting | bytes 134217728 | tf_op jit(solution)/shard_map/reshape;squeeze | solution.py:53
  44.4 0.0 copy-start.2
  44.4 0.0 copy-start.3
  44.4 0.0 copy-start.4
  44.5 13.1 all-to-all-start
  57.6 0.0 copy-done.2
  57.6 0.0 copy-done.3
  57.7 0.1 copy.34
  57.8 0.2 reshape.200
  57.9 0.0 copy-done.4
  58.0 0.1 copy.35
  58.1 722.5 %all-to-all-done = bf16[1,32,4,64,4096]{4,3,1,0,2:T(8,128)(2,1)} async-done(((bf16[1,32,4,64,4096]{4,3,1,0,2:T(8,128)(2,1)}), bf16[1,32,4,64,4096]{4,3,1,0,2:T(8,128)(2,1)}, u32[]{:S(2)}, u32[]{:S(2)}) %all-to-all-start) | async-done | bytes 67108896 | tf_op jit(solution)/shard_map/all_to_all | solution.py:54
  780.6 133.7 %gather_fusion = bf16[4096,4096]{1,0:T(8,128)(2,1)} fusion(bf16[1,8192,4096]{2,1,0:T(8,128)(2,1)} %bitcast.4, s32[4096]{0:T(1024)S(1)} %reshape.200), kind=kCustom, calls=%fused_computation | custom fusion | bytes 67141632 | tf_op jit(solution)/shard_map/vmap(jit(_take))/gather | solution.py:10
  914.4 32.5 %fusion.10 = f32[512,4096]{1,0:T(8,128)} fusion(bf16[4096,4096]{1,0:T(8,128)(2,1)} %gather_fusion, f32[512,8]{1,0:T(8,128)S(1)} %copy.35), kind=kLoop, calls=%fused_computation.15 | loop fusion | flops 48234496 | bytes 41959424 | tf_op jit(solution)/shard_map/reduce_sum | solution.py:15
  946.9 0.0 copy-start.5
  946.9 5.9 fusion.35
  952.8 2.4 collective-permute-start
  955.2 0.8 iota_compare_fusion
  956.0 89.7 %collective-permute-done = bf16[1,1,512,4096]{3,2,1,0:T(8,128)(2,1)S(1)} collective-permute-done((bf16[1,1,512,4096]{3,2,1,0:T(8,128)(2,1)S(1)}, bf16[1,1,512,4096]{3,2,1,0:T(8,128)(2,1)S(1)}, u32[]{:S(2)}, u32[]{:S(2)}) %collective-permute-start) | collective-permute-done | bytes 4194336 | tf_op jit(solution)/shard_map/ppermute | solution.py:62
  1045.7 0.0 copy-start
  1045.7 2.0 copy-done
  1047.7 0.9 fusion.31
  1048.6 0.0 copy-done.5
  1048.6 61.9 %fusion.15 = bf16[512,12288]{1,0:T(8,128)(2,1)} fusion(bf16[1,4096,12288]{2,1,0:T(8,128)(2,1)} %param.18, bf16[1,1,512,4096]{3,2,1,0:T(8,128)(2,1)} %copy-done, f32[4096]{0:T(1024)S(1)} %bitcast.121, f32[512]{0:T(512)S(1)} %add_rsqrt_fusion), kind=kOutput, calls=%fused_computation.20 | convolution fusion | flops 51554287616 | bytes 117458944 | tf_op jit(solution)/shard_map/mbld,de->mble/dot_general | solution.py:28
  1110.5 16.7 %copy.43 = bf16[512,12288]{0,1:T(8,128)(2,1)} copy(bf16[512,12288]{1,0:T(8,128)(2,1)} %fusion.15) | data formatting | bytes 25165824 | tf_op jit(solution)/shard_map/reshape.19
  1127.2 61.6 %fusion.48 = bf16[64,96,8,128]{3,2,1,0:T(8,128)(2,1)} fusion(bf16[1,4096,12288]{2,1,0:T(8,128)(2,1)} %param.16, bf16[1,1,512,4096]{3,2,1,0:T(8,128)(2,1)} %copy-done, f32[4096]{0:T(1024)S(1)} %bitcast.122, f32[512]{0:T(512)S(1)} %add_rsqrt_fusion), kind=kOutput, calls=%fused_computation.42 | convolution fusion | flops 51554287616 | bytes 117458944 | tf_op jit(solution)/shard_map/mbld,de->mble/dot_general | solution.py:28
  1188.8 61.8 %fusion.45 = bf16[64,96,8,128]{3,2,1,0:T(8,128)(2,1)} fusion(bf16[1,4096,12288]{2,1,0:T(8,128)(2,1)} %param.17, bf16[1,1,512,4096]{3,2,1,0:T(8,128)(2,1)} %copy-done, f32[4096]{0:T(1024)S(1)} %bitcast.123, f32[512]{0:T(512)S(1)} %add_rsqrt_fusion), kind=kOutput, calls=%fused_computation.41 | convolution fusion | flops 51554287616 | bytes 117458944 | tf_op jit(solution)/shard_map/mbld,de->mble/dot_general | solution.py:28
  1250.6 0.0 copy-start.1
  1250.6 43.6 %fusion.24 = f32[96,512,512]{1,2,0:T(8,128)} fusion(bf16[64,96,8,128]{3,2,1,0:T(8,128)(2,1)} %fusion.45, bf16[64,96,8,128]{3,2,1,0:T(8,128)(2,1)} %fusion.48), kind=kOutput, calls=%fused_computation.23 | convolution fusion | flops 6442450944 | bytes 125829120 | tf_op jit(solution)/shard_map/mbqhe,mbkhe->mbhqk/dot_general | solution.py:33
  1294.1 0.0 copy-done.1
  1294.1 97.1 %fusion.69 = (f32[96,512]{1,0:T(8,128)S(1)}, f32[96,512,512]{1,2,0:T(8,128)}) fusion(f32[96,512,512]{1,2,0:T(8,128)} %fusion.24, pred[512,512]{0,1:T(8,128)(4,1)S(1)} %copy-done.1), kind=kOutput, calls=%fused_computation.58 | output fusion | flops 150995456 | bytes 201785344 | tf_op jit(solution)/shard_map/sub | solution.py:36
  1391.3 40.1 %fusion.83 = bf16[512,96,128]{0,2,1:T(8,128)(2,1)} fusion(bf16[512,96,128]{0,2,1:T(8,128)(2,1)} %bitcast.120, f32[96,512,512]{1,2,0:T(8,128)} %get-tuple-element.6, f32[96,512]{1,0:T(8,128)S(1)} %get-tuple-element.5), kind=kOutput, calls=%fused_computation.28.clone.clone.clone.clone.clone.clone.clone.clone.clone.1 | convolution fusion | flops 6499074048 | bytes 126025728 | tf_op jit(solution)/shard_map/mbhqk,mbkhe->mbqhe/dot_general | solution.py:37
  1431.4 62.6 %fusion.55 = bf16[1,1,1,512,4096]{4,3,2,1,0:T(8,128)(2,1)} fusion(bf16[1,96,128,4096]{3,2,1,0:T(8,128)(2,1)} %param.19, bf16[1,1,512,4096]{3,2,1,0:T(8,128)(2,1)} %copy-done, bf16[512,96,128]{0,2,1:T(8,128)(2,1)} %fusion.83), kind=kOutput, calls=%fused_computation.43 | convolution fusion | flops 51550093312 | bytes 121634816 | tf_op jit(solution)/shard_map/mbqhe,hed->mbqd/dot_general | solution.py:38
  (5 shorter events, 0.0 us)
Async XLA Ops:
  44.4 13.2 copy-start.2
  44.4 13.2 copy-start.3
  44.4 13.5 copy-start.4
  44.5 736.2 %all-to-all-start = ((bf16[1,32,4,64,4096]{4,3,1,0,2:T(8,128)(2,1)}), bf16[1,32,4,64,4096]{4,3,1,0,2:T(8,128)(2,1)}, u32[]{:S(2)}, u32[]{:S(2)}) async-start(bf16[1,32,4,64,4096]{4,3,1,0,2:T(8,128)(2,1)} %copy.33), calls=%async_computation | async-start | bytes 134217728 | tf_op jit(solution)/shard_map/all_to_all | solution.py:54
  946.9 101.7 %copy-start.5 = (f32[1,4096]{1,0:T(1,128)S(1)}, f32[1,4096]{1,0:T(1,128)}, u32[]{:S(2)}) copy-start(f32[1,4096]{1,0:T(1,128)} %param.15) | copy-start | bytes 49156
  952.8 92.9 %collective-permute-start = (bf16[1,1,512,4096]{3,2,1,0:T(8,128)(2,1)S(1)}, bf16[1,1,512,4096]{3,2,1,0:T(8,128)(2,1)S(1)}, u32[]{:S(2)}, u32[]{:S(2)}) collective-permute-start(bf16[1,1,512,4096]{3,2,1,0:T(8,128)(2,1)S(1)} %fusion.35), channel_id=1, source_target_pairs={{0,4},{4,0},{1,5},{5,1},{2,6},{6,2},{3,7},{7,3}} | collective-permute-start | bytes 12582920 | tf_op jit(solution)/shard_map/ppermute | solution.py:62
  1045.7 2.0 copy-start
  1250.6 43.6 %copy-start.1 = (pred[512,512]{0,1:T(8,128)(4,1)S(1)}, pred[512,512]{0,1:T(8,128)(4,1)}, u32[]{:S(2)}) copy-start(pred[512,512]{0,1:T(8,128)(4,1)} %iota_compare_fusion) | copy-start | bytes 786436
where the time goes:
time: 1500 us; the launch traced here: 1490 us
  waiting for transfers between devices  812 us (54%)
  matrix products  332 us (22%)
  local copies, waits for them, and re-layouts  197 us (13%)
  other arithmetic  137 us (9%)
  starting transfers between devices  15.6 us (1%)
    all_to_all x1, waiting for transfers between devices, local_step(): received = lax.all_to_all(split_view, 'ep', 2, 1, tiled=True)  723 us
    dot_general x3, matrix products, project(): jnp.einsum('mbld,de->mble', normed, w_mat, preferred_element_type=jnp.flo...  185 us
    gather x4, local copies, waits for them, and re-layouts, take_rows(): return jnp.take(row_table, flat_ids, axis=0, mode='clip')  134 us
    sub x1, other arithmetic, attend_block(): jax.nn.softmax(jnp.where(causal, scores, -jnp.inf), axis=-1)  97.1 us
    ppermute x1, waiting for transfers between devices, local_step(): arrived = lax.ppermute(combined, 'pp', shift_pairs)  89.7 us
    dot_general x1, matrix products, attend_block(): jnp.einsum('mbqhe,hed->mbqd', context, w_out, preferred_element_type=jnp....  62.6 us
    another operation x1, local copies, waits for them, and re-layouts, local_step(): own_out.reshape(micro_count, local_experts, ep_size, slot_dev, model_dim)  44.4 us
    dot_general x1, matrix products, attend_block(): jnp.einsum('mbqhe,mbkhe->mbhqk', q_heads, k_heads, preferred_element_type...  43.6 us
  transfers between devices with their start and end apart: 2, of which 2 were waited for; matrix products, arithmetic and copies ran while one was open for 0% of the time, Pallas kernels for 0%

commit v1 on v0

v1 whole, which is shorter than its diff:
```python
import functools

import jax
import jax.numpy as jnp
from jax import lax
from jax.experimental import pallas as pl
from jax.experimental.pallas import tpu as pltpu
from jax.sharding import PartitionSpec as P

NORM_EPS = 1e-6
LANES = 128
VMEM_LIMIT = 62 * 2**20
PART_COLS = 512
SEND_COLS = 1024
HEAD_GROUP = 2
WEIGHT_BUFFERS = 3
HALVES = 2
ANY_SPEC = pl.BlockSpec(memory_space=pl.ANY)
VMEM_SPEC = pl.BlockSpec(memory_space=pltpu.VMEM)


def fill_gate_terms(table_ref, first_row, first_code, terms_ref):
    rows = terms_ref.shape[0] // 3
    slots = terms_ref.shape[1]
    top_k = table_ref.shape[1] // 2
    step = 32

    @pl.loop(0, rows // step)
    def _(i):
        table = table_ref[pl.ds(pl.multiple_of(first_row + i * step, step), step), :]
        lane_ids = lax.broadcasted_iota(jnp.int32, (step, LANES), 1).astype(jnp.float32)
        codes = [jnp.broadcast_to(table[:, j:j + 1] - first_code, (step, LANES)) for j in range(top_k)]
        gates = [jnp.broadcast_to(table[:, top_k + j:top_k + j + 1], (step, LANES)) for j in range(top_k)]
        for tile in range(slots // LANES):
            here = lane_ids + float(tile * LANES)
            gate = jnp.zeros((step, LANES), jnp.float32)
            for j in range(top_k):
                gate = jnp.where(codes[j] == here, gates[j], gate)
            high = gate.astype(jnp.bfloat16)
            rest = gate - high.astype(jnp.float32)
            middle = rest.astype(jnp.bfloat16)
            low = (rest - middle.astype(jnp.float32)).astype(jnp.bfloat16)
            for k, term in enumerate((high, middle, low)):
                at = pl.ds(pl.multiple_of(k * rows + i * step, step), step)
                terms_ref[at, tile * LANES:(tile + 1) * LANES] = term


def normalise(x_ref, gain_ref, normed_ref):
    for first in range(0, x_ref.shape[0], 64):
        x_float = x_ref[first:first + 64].astype(jnp.float32)
        inv_rms = lax.rsqrt(jnp.mean(jnp.square(x_float), axis=-1, keepdims=True) + NORM_EPS)
        normed_ref[first:first + 64] = (x_float * inv_rms * gain_ref[...]).astype(jnp.bfloat16)


def attend_heads(queries, key_parts, value_parts, head_dim, out_ref):
    rows = queries.shape[0]
    scale = head_dim ** -0.5
    q_pos = lax.broadcasted_iota(jnp.int32, (rows, rows), 0)
    k_pos = lax.broadcasted_iota(jnp.int32, (rows, rows), 1)
    causal = q_pos >= k_pos
    for first in range(0, queries.shape[1], head_dim):
        cols = slice(first, first + head_dim)
        query = queries[:, cols]
        scores = [
            lax.dot_general(query, keys[:, cols], (((1,), (1,)), ((), ())), preferred_element_type=jnp.float32) * scale
            for keys in key_parts
        ]
        scores[-1] = jnp.where(causal, scores[-1], -jnp.inf)
        top = scores[0].max(axis=-1, keepdims=True)
        for s in scores[1:]:
            top = jnp.maximum(top, s.max(axis=-1, keepdims=True))
        weights = [jnp.exp(s - top) for s in scores]
        total = weights[0].sum(axis=-1, keepdims=True)
        for w in weights[1:]:
            total = total + w.sum(axis=-1, keepdims=True)
        inverse = 1.0 / total
        mixed = jnp.zeros((rows, head_dim), jnp.float32)
        for w, values in zip(weights, value_parts):
            mixed = mixed + jnp.dot((w * inverse).astype(jnp.bfloat16), values[:, cols], preferred_element_type=jnp.float32)
        out_ref[:, cols] = mixed.astype(jnp.bfloat16)


def project_block(normed_ref, w_ref):
    return jnp.dot(normed_ref[...], w_ref[...], preferred_element_type=jnp.float32).astype(jnp.bfloat16)


def weight_spec_at(model_dim, cols, first):
    return pl.BlockSpec((model_dim, cols), lambda n: (0, n + first), pipeline_mode=pl.Buffered(WEIGHT_BUFFERS))


def exchange_kernel(head_dim, table_ref, out_rows_ref, resid_ref, gain_ref, wq_ref, wk_ref, wv_ref,
                    arrived_ref, k_ref, v_ref, context_ref, pair_out_ref, cross_out_ref, near_out_ref,
                    terms_ref, pair_in_ref, near_in_ref, cross_in_ref, base_ref, combined_ref, x_ref, normed_ref,
                    load_sem, send_sems, recv_sems):
    me = lax.axis_index('ep')
    stage = lax.axis_index('pp')
    seq, model_dim = resid_ref.shape
    half = seq // HALVES
    experts = out_rows_ref.shape[0]
    slot_dev = out_rows_ref.shape[1] // table_ref.shape[0]
    first_code = (me * (experts * slot_dev)).astype(jnp.float32)
    partner, across, diagonal = me ^ 1, me ^ 2, me ^ 3
    next_stage = 1 - stage

    barrier = pltpu.get_barrier_semaphore()
    pl.semaphore_signal(barrier, inc=1, device_id={'ep': partner}, device_id_type=pl.DeviceIdType.MESH)
    pl.semaphore_signal(barrier, inc=1, device_id={'ep': across}, device_id_type=pl.DeviceIdType.MESH)
    pl.semaphore_signal(barrier, inc=1, device_id={'pp': next_stage}, device_id_type=pl.DeviceIdType.MESH)
    pl.semaphore_wait(barrier, 3)

    copies = []

    def send(src_ref, dst_ref, target):
        index = len(copies)
        copy = pltpu.make_async_remote_copy(
            src_ref=src_ref, dst_ref=dst_ref, send_sem=send_sems.at[index], recv_sem=recv_sems.at[index],
            device_id=target, device_id_type=pl.DeviceIdType.MESH)
        copy.start()
        copies.append(copy)
        return copy

    def fill(slot, owner, part):
        fill_gate_terms(table_ref.at[owner], part * half, first_code, terms_ref.at[slot])

    def partial_sums(slot, owner, first, cols, dst_ref, extra_ref=None, resid=None, keep_ref=None):
        steps, begin = cols // PART_COLS, first // PART_COLS

        def body(block_ref, *refs):
            block = block_ref[...].reshape(experts * slot_dev, PART_COLS)
            sums = jnp.dot(terms_ref[slot], block, preferred_element_type=jnp.float32)
            total = sums[:half] + (sums[half:2 * half] + sums[2 * half:])
            at = pl.ds(pl.multiple_of((pl.program_id(0) + begin) * PART_COLS, PART_COLS), PART_COLS)
            if extra_ref is not None:
                total = total + extra_ref[:, at]
            if resid is not None:
                total = refs[0][...].astype(jnp.float32) + total
            if keep_ref is not None:
                keep_ref[:, at] = total
            else:
                refs[-1][...] = total

        col_spec = pl.BlockSpec((half, PART_COLS), lambda n: (0, n + begin))
        in_specs = [pl.BlockSpec((experts, slot_dev, PART_COLS), lambda n: (0, owner, n + begin))]
        operands = [out_rows_ref]
        if resid is not None:
            in_specs.append(col_spec)
            operands.append(resid)
        if keep_ref is None:
            pltpu.emit_pipeline(body, grid=(steps,), in_specs=in_specs, out_specs=[col_spec])(*operands, dst_ref)
        else:
            pltpu.emit_pipeline(body, grid=(steps,), in_specs=in_specs)(*operands)

    def col_span(first, cols):
        return (slice(None), pl.ds(first, cols))

    def half_rows(part):
        return pl.ds(part * half, half)

    def pair_part(part, first, cols):
        source = pair_out_ref.at[part]
        partial_sums(0, diagonal, first, cols, source)
        span = col_span(first, cols)
        return send(source.at[span], pair_in_ref.at[span], {'ep': partner})

    def cross_part(part, first, cols, pair):
        pair.wait_recv()
        source = cross_out_ref.at[part]
        partial_sums(1, across, first, cols, source, extra_ref=pair_in_ref)
        for at in range(first, first + cols, SEND_COLS):
            span = col_span(at, SEND_COLS)
            crossed[part].append(send(source.at[span], cross_in_ref.at[part].at[span], {'ep': across}))

    def near_part(part):
        source = near_out_ref.at[part]
        partial_sums(0, partner, 0, model_dim, source)
        return send(source, near_in_ref, {'ep': partner})

    def base_part(part, near):
        near.wait_recv()
        partial_sums(1, me, 0, model_dim, None, extra_ref=near_in_ref, resid=resid_ref.at[half_rows(part)], keep_ref=base_ref)

    def finish(part, index):
        if part > 0:
            moved[part - 1][index].wait_send()
        crossed[part][index].wait_recv()
        span = col_span(index * SEND_COLS, SEND_COLS)
        combined_ref[span] = (base_ref[span] + cross_in_ref[(part,) + span]).astype(jnp.bfloat16)
        target = arrived_ref.at[half_rows(part), pl.ds(index * SEND_COLS, SEND_COLS)]
        moved[part].append(send(combined_ref.at[span], target, {'pp': next_stage}))

    crossed = [[], []]
    moved = [[], []]
    chunks = model_dim // SEND_COLS
    one, rest = SEND_COLS, model_dim - 2 * SEND_COLS
    fill(0, diagonal, 0)
    pair_a = pair_part(0, 0, one)
    fill(1, across, 0)
    cross_part(0, 0, one, pair_a)
    pair_b = pair_part(0, one, one)
    pair_c = pair_part(0, 2 * one, rest)
    cross_part(0, one, one, pair_b)
    cross_part(0, 2 * one, rest, pair_c)
    fill(0, partner, 0)
    near = near_part(0)
    fill(1, me, 0)
    base_part(0, near)
    finish(0, 0)
    finish(0, 1)
    fill(0, diagonal, 1)
    pair_d = pair_part(1, 0, model_dim)
    finish(0, 2)
    fill(1, across, 1)
    cross_part(1, 0, model_dim, pair_d)
    for index in range(3, chunks):
        finish(0, index)
    fill(0, partner, 1)
    near = near_part(1)
    fill(1, me, 1)

    for copy in moved[0]:
        copy.wait_recv()
    load = pltpu.make_async_copy(arrived_ref.at[half_rows(0)], x_ref, load_sem)
    load.start()
    load.wait()
    normalise(x_ref, gain_ref, normed_ref)

    group = HEAD_GROUP * head_dim
    groups = k_ref.shape[1] // group

    def head_groups(first, count):
        def body(wq_block, wk_block, wv_block, k_block, v_block, context_block):
            queries, keys, values = [project_block(normed_ref, w) for w in (wq_block, wk_block, wv_block)]
            k_block[...] = keys
            v_block[...] = values
            attend_heads(queries, [keys], [values], head_dim, context_block)

        out_spec = pl.BlockSpec((half, group), lambda n: (0, n + first))
        pltpu.emit_pipeline(
            body, grid=(count,), in_specs=[weight_spec_at(model_dim, group, first)] * 3, out_specs=[out_spec] * 3,
        )(wq_ref, wk_ref, wv_ref, k_ref, v_ref, context_ref.at[half_rows(0)])

    third = groups // 3
    head_groups(0, third)
    base_part(1, near)
    finish(1, 0)
    finish(1, 1)
    head_groups(third, third)
    for index in range(2, chunks):
        finish(1, index)
    head_groups(2 * third, groups - 2 * third)
    for copy in moved[1]:
        copy.wait_recv()
    already = {id(copy) for copy in moved[0]}
    for copy in copies:
        if id(copy) not in already:
            copy.wait_send()


def exchange(table, own_out, own_resid, gain, w_query, w_key, w_value, head_dim):
    seq, model_dim = own_resid.shape
    hidden = w_query.shape[1]
    half = seq // HALVES
    slots = own_out.shape[0] * own_out.shape[1] // table.shape[0]
    staged = jax.ShapeDtypeStruct((HALVES, half, model_dim), jnp.float32)
    out_shape = [
        jax.ShapeDtypeStruct((seq, model_dim), jnp.bfloat16),
        jax.ShapeDtypeStruct((half, hidden), jnp.bfloat16),
        jax.ShapeDtypeStruct((half, hidden), jnp.bfloat16),
        jax.ShapeDtypeStruct((seq, hidden), jnp.bfloat16),
        staged, staged, staged,
    ]
    chunks = model_dim // SEND_COLS
    n_copies = 4 + 2 + 2 * HALVES * chunks
    outs = pl.pallas_call(
        functools.partial(exchange_kernel, head_dim),
        out_shape=out_shape,
        in_specs=[VMEM_SPEC, ANY_SPEC, ANY_SPEC, VMEM_SPEC, ANY_SPEC, ANY_SPEC, ANY_SPEC],
        out_specs=[ANY_SPEC] * len(out_shape),
        scratch_shapes=[
            pltpu.VMEM((2, 3 * half, slots), jnp.bfloat16),
            pltpu.VMEM((half, model_dim), jnp.float32),
            pltpu.VMEM((half, model_dim), jnp.float32),
            pltpu.VMEM((HALVES, half, model_dim), jnp.float32),
            pltpu.VMEM((half, model_dim), jnp.float32),
            pltpu.VMEM((half, model_dim), jnp.bfloat16),
            pltpu.VMEM((half, model_dim), jnp.bfloat16),
            pltpu.VMEM((half, model_dim), jnp.bfloat16),
            pltpu.SemaphoreType.DMA,
            pltpu.SemaphoreType.DMA((n_copies,)),
            pltpu.SemaphoreType.DMA((n_copies,)),
        ],
        compiler_params=pltpu.CompilerParams(vmem_limit_bytes=VMEM_LIMIT, collective_id=0, has_side_effects=True),
        name="exchange",
    )(table, own_out, own_resid, gain, w_query, w_key, w_value)
    return outs[:4]


def second_half_kernel(head_dim, gain_ref, x_ref, wq_ref, wk_ref, wv_ref, k_ref, v_ref, held_ref, context_ref, normed_ref):
    del held_ref
    half, model_dim = x_ref.shape
    normalise(x_ref, gain_ref, normed_ref)
    group = HEAD_GROUP * head_dim
    groups = k_ref.shape[1] // group

    def body(wq_block, wk_block, wv_block, k_block, v_block, context_block):
        queries, keys, values = [project_block(normed_ref, w) for w in (wq_block, wk_block, wv_block)]
        attend_heads(queries, [k_block[...], keys], [v_block[...], values], head_dim, context_block)

    spec = pl.BlockSpec((half, group), lambda n: (0, n))
    pltpu.emit_pipeline(
        body, grid=(groups,), in_specs=[weight_spec_at(model_dim, group, 0)] * 3 + [spec] * 2, out_specs=[spec],
    )(wq_ref, wk_ref, wv_ref, k_ref, v_ref, context_ref.at[pl.ds(half, half)])


def second_half(arrived, gain, w_query, w_key, w_value, keys, values, context, head_dim):
    seq, model_dim = arrived.shape
    hidden = w_query.shape[1]
    half = seq // HALVES
    return pl.pallas_call(
        functools.partial(second_half_kernel, head_dim),
        out_shape=jax.ShapeDtypeStruct(context.shape, context.dtype),
        grid=(1,),
        in_specs=[pl.BlockSpec(gain.shape, lambda n: (0, 0)), pl.BlockSpec((half, model_dim), lambda n: (1, 0))] + [ANY_SPEC] * 6,
        out_specs=ANY_SPEC,
        input_output_aliases={7: 0},
        scratch_shapes=[pltpu.VMEM((half, model_dim), jnp.bfloat16)],
        compiler_params=pltpu.CompilerParams(vmem_limit_bytes=VMEM_LIMIT, dimension_semantics=("arbitrary",)),
        cost_estimate=pl.CostEstimate(flops=6 * half * model_dim * hidden, bytes_accessed=6 * model_dim * hidden, transcendentals=0),
        name="second_half",
    )(gain, arrived, w_query, w_key, w_value, keys, values, context)


def solution(mesh):
    ep_size = mesh.shape['ep']
    token_spec = P(('data', 'pp'), None, 'ep', None, None)
    weight_spec = P('pp', None, None)

    def local_step(expert_out, expert_ids, slot_ids, gates, resid, norm_scale, w_query, w_key, w_value, w_out):
        own_out = expert_out[0, 0]
        own_resid = resid[0, 0, 0]
        model_dim = own_out.shape[2]
        slot_dev = own_out.shape[1] // ep_size
        me = lax.axis_index('ep')
        ids, slots, own_gates = expert_ids[0, 0, 0], slot_ids[0, 0, 0], gates[0, 0, 0]
        code = jnp.where(slots >= 0, ids * slot_dev + (slots - me * slot_dev), -1).astype(jnp.float32)
        own_table = jnp.concatenate([code.T, own_gates.T], axis=0)
        table = lax.all_gather(own_table, 'ep').transpose(0, 2, 1)
        gain = norm_scale.reshape(1, model_dim)
        head_count, head_dim = w_out.shape[1], w_out.shape[2]
        weights = (w_query[0], w_key[0], w_value[0])
        arrived, keys, values, context = exchange(table, own_out, own_resid, gain, *weights, head_dim)
        context = second_half(arrived, gain, *weights, keys, values, context, head_dim)
        flat_out = w_out[0].reshape(head_count * head_dim, model_dim)
        proj = jnp.dot(context, flat_out, preferred_element_type=jnp.float32).astype(jnp.bfloat16)
        result = (arrived.astype(jnp.float32) + proj.astype(jnp.float32)).astype(jnp.bfloat16)
        return result[None, None, None]

    return jax.shard_map(local_step, mesh=mesh, in_specs=(token_spec, token_spec, token_spec, token_spec, token_spec, P('pp', None), weight_spec, weight_spec, weight_spec, P('pp', None, None, None)), out_specs=token_spec, check_vma=False)
```

time: 1500 us -> 549 us (0.37)
  waiting for transfers between devices: 812 us -> 0 us
  Pallas kernels: 0 us -> 473 us
  matrix products: 332 us -> 62.4 us
  local copies, waits for them, and re-layouts: 197 us -> 1.31 us
  other arithmetic: 137 us -> 1.46 us
  starting transfers between devices: 15.6 us -> 0 us
    all_to_all x1 -> x0, waiting for transfers between devices: 723 us -> none  [local_step(): received = lax.all_to_all(split_view, 'ep', 2, 1, tiled=True)]
    pallas_call x0 -> x2, Pallas kernels: none -> 473 us  [the longest x1 326 us: exchange(): pl.pallas_call(functools.partial(exchange_kernel, head_dim), out_shape=ou...]
    dot_general x6 -> x1, matrix products: 332 us -> 62.4 us  [local_step(): jnp.dot(context, flat_out, preferred_element_type=jnp.float32)]
    gather x4 -> x0, local copies, waits for them, and re-layouts: 134 us -> none  [take_rows(): return jnp.take(row_table, flat_ids, axis=0, mode='clip')]
    sub x1 -> x0, other arithmetic: 97.1 us -> none  [attend_block(): jax.nn.softmax(jnp.where(causal, scores, -jnp.inf), axis=-1)]
    ppermute x1 -> x0, waiting for transfers between devices: 89.7 us -> none  [local_step(): arrived = lax.ppermute(combined, 'pp', shift_pairs)]
    another operation x2 -> x0, local copies, waits for them, and re-layouts: 61.1 us -> none  [the longest x1 44.4 us: local_step(): own_out.reshape(micro_count, local_experts, ep_size, slot_dev, model_dim)]
    reduce_sum x2 -> x0, other arithmetic: 33.4 us -> none  [the longest x1 32.5 us: combine_rows(): mixed = jnp.sum(gathered.astype(jnp.float32) * weights[..., None], axis=3)]
  transfers between devices with their start and end apart: 2 -> 0, of which waited for: 2 -> 0; matrix products, arithmetic and copies ran while one was open for 0% -> 0% of each run, Pallas kernels for 0% -> 0%
where the time goes in v1:
time: 549 us
  Pallas kernels  473 us (86%)
  matrix products  62.4 us (11%)
  blocking collectives  10.3 us (2%)
    pallas_call x1, Pallas kernels, exchange(): pl.pallas_call(functools.partial(exchange_kernel, head_dim), out_shape=ou...  326 us
    pallas_call x1, Pallas kernels, second_half(): pl.pallas_call(functools.partial(second_half_kernel, head_dim), out_shape...  147 us
    dot_general x1, matrix products, local_step(): jnp.dot(context, flat_out, preferred_element_type=jnp.float32)  62.4 us

profile of v1, /device:TPU:0, one launch (start us, length us, event | category | flops | bytes accessed | tf_op | source)
XLA Modules:
  0.0 548.5 jit_solution(5522118422944346161)
XLA Ops:
  0.0 0.7 convert_bitcast_fusion
  0.7 0.7 pad_maximum_fusion
  1.5 10.3 %all-gather = f32[64,512]{1,0:T(8,128)S(1)} all-gather(f32[16,512]{1,0:T(8,128)S(1)} %pad_maximum_fusion), channel_id=2, replica_groups=mesh['data'=1,'pp'=2,'ep'=4] {'ep'}, dimensions={0}, use_global_device_ids=true | all-gather | bytes 163840 | tf_op jit(solution)/shard_map/all_gather | solution.py:347
  11.7 1.3 copy.12
  13.0 326.1 %exchange.1 = (bf16[512,4096]{1,0:T(8,128)(2,1)}, bf16[256,12288]{1,0:T(8,128)(2,1)}, bf16[256,12288]{1,0:T(8,128)(2,1)}, bf16[512,12288]{1,0:T(8,128)(2,1)}, f3...) custom-call(f32[4,512,16]{2,1,0:T(8,128)} %bitcast.20, ...), custom_call_target="tpu_custom_call" | custom-call | tf_op jit(solution)/shard_map/exchange/pallas_call | solution.py:274
  339.1 147.0 %second_half.1 = bf16[512,12288]{1,0:T(8,128)(2,1)} custom-call(f32[1,4096]{1,0:T(1,128)} %gain_ref.3, bf16[512,4096]{1,0:T(8,128)(2,1)} %get-tuple-element.9.x_ref, bf16[4096,12288]{1,0:T(8,128)(2,1)} %bitcast.8.wq_ref, bf16[4096,12288]{1,0:T(8,128)(2,1)} %bitcast.9.wk_ref, bf16[4096,12288]{1,0:T(8,128)(2,1)} %bitcast.10.wv_ref, ...), custom_call_target="tpu_custom_call", output_to_operand_aliasing={{}: (7, {})} | custom-call | flops 77309411328 | bytes 301989888 | tf_op jit(solution)/shard_map/second_half/pallas_call | solution.py:319
  486.1 62.4 %fusion = bf16[1,1,1,512,4096]{4,3,2,1,0:T(8,128)(2,1)} fusion(bf16[512,12288]{1,0:T(8,128)(2,1)} %second_half.1, bf16[12288,4096]{1,0:T(8,128)(2,1)} %bitcast.11, bf16[512,4096]{1,0:T(8,128)(2,1)} %get-tuple-element.9.x_ref), kind=kOutput, calls=%fused_computation.2 | convolution fusion | flops 51550093312 | bytes 121634816 | tf_op jit(solution)/shard_map/dot_general | solution.py:354

commit v2 on v1

--- a/solution.py
+++ b/solution.py
@@ -15,25 +15,28 @@
 HEAD_GROUP = 2
 WEIGHT_BUFFERS = 3
 HALVES = 2
+FILL_ROWS = 32
+FILL_STEP = 16
+GATE_SLOTS = 3
+QUERY_ROWS = 128
+LOG2_E = 1.4426950408889634
 ANY_SPEC = pl.BlockSpec(memory_space=pl.ANY)
 VMEM_SPEC = pl.BlockSpec(memory_space=pltpu.VMEM)
 
 
-def fill_gate_terms(table_ref, first_row, first_code, terms_ref):
+def fill_gate_block(table_ref, first_row, first_code, terms_ref, block):
     rows = terms_ref.shape[0] // 3
     slots = terms_ref.shape[1]
     top_k = table_ref.shape[1] // 2
-    step = 32
-
-    @pl.loop(0, rows // step)
-    def _(i):
-        table = table_ref[pl.ds(pl.multiple_of(first_row + i * step, step), step), :]
-        lane_ids = lax.broadcasted_iota(jnp.int32, (step, LANES), 1).astype(jnp.float32)
-        codes = [jnp.broadcast_to(table[:, j:j + 1] - first_code, (step, LANES)) for j in range(top_k)]
-        gates = [jnp.broadcast_to(table[:, top_k + j:top_k + j + 1], (step, LANES)) for j in range(top_k)]
+    lane_ids = lax.broadcasted_iota(jnp.int32, (FILL_STEP, LANES), 1).astype(jnp.float32)
+    for first in range(0, FILL_ROWS, FILL_STEP):
+        begin = block * FILL_ROWS + first
+        table = table_ref[pl.ds(pl.multiple_of(first_row + begin, FILL_STEP), FILL_STEP), :]
+        codes = [jnp.broadcast_to(table[:, j:j + 1] - first_code, (FILL_STEP, LANES)) for j in range(top_k)]
+        gates = [jnp.broadcast_to(table[:, top_k + j:top_k + j + 1], (FILL_STEP, LANES)) for j in range(top_k)]
         for tile in range(slots // LANES):
             here = lane_ids + float(tile * LANES)
-            gate = jnp.zeros((step, LANES), jnp.float32)
+            gate = jnp.zeros((FILL_STEP, LANES), jnp.float32)
             for j in range(top_k):
                 gate = jnp.where(codes[j] == here, gates[j], gate)
             high = gate.astype(jnp.bfloat16)
@@ -41,7 +44,7 @@
             middle = rest.astype(jnp.bfloat16)
             low = (rest - middle.astype(jnp.float32)).astype(jnp.bfloat16)
             for k, term in enumerate((high, middle, low)):
-                at = pl.ds(pl.multiple_of(k * rows + i * step, step), step)
+                at = pl.ds(pl.multiple_of(k * rows + begin, FILL_STEP), FILL_STEP)
                 terms_ref[at, tile * LANES:(tile + 1) * LANES] = term
 
 
@@ -52,32 +55,38 @@
         normed_ref[first:first + 64] = (x_float * inv_rms * gain_ref[...]).astype(jnp.bfloat16)
 
 
-def attend_heads(queries, key_parts, value_parts, head_dim, out_ref):
-    rows = queries.shape[0]
-    scale = head_dim ** -0.5
-    q_pos = lax.broadcasted_iota(jnp.int32, (rows, rows), 0)
-    k_pos = lax.broadcasted_iota(jnp.int32, (rows, rows), 1)
+def attend_heads(q_ref, key_refs, value_refs, head_dim, out_ref):
+    rows = q_ref.shape[0]
+    scale = head_dim ** -0.5 * LOG2_E
+    q_pos = lax.broadcasted_iota(jnp.int32, (QUERY_ROWS, QUERY_ROWS), 0)
+    k_pos = lax.broadcasted_iota(jnp.int32, (QUERY_ROWS, QUERY_ROWS), 1)
     causal = q_pos >= k_pos
-    for first in range(0, queries.shape[1], head_dim):
+    for first in range(0, q_ref.shape[1], head_dim):
         cols = slice(first, first + head_dim)
-        query = queries[:, cols]
-        scores = [
-            lax.dot_general(query, keys[:, cols], (((1,), (1,)), ((), ())), preferred_element_type=jnp.float32) * scale
-            for keys in key_parts
-        ]
-        scores[-1] = jnp.where(causal, scores[-1], -jnp.inf)
-        top = scores[0].max(axis=-1, keepdims=True)
-        for s in scores[1:]:
-            top = jnp.maximum(top, s.max(axis=-1, keepdims=True))
-        weights = [jnp.exp(s - top) for s in scores]
-        total = weights[0].sum(axis=-1, keepdims=True)
-        for w in weights[1:]:
-            total = total + w.sum(axis=-1, keepdims=True)
-        inverse = 1.0 / total
-        mixed = jnp.zeros((rows, head_dim), jnp.float32)
-        for w, values in zip(weights, value_parts):
-            mixed = mixed + jnp.dot((w * inverse).astype(jnp.bfloat16), values[:, cols], preferred_element_type=jnp.float32)
-        out_ref[:, cols] = mixed.astype(jnp.bfloat16)
+        for start in range(0, rows, QUERY_ROWS):
+            here = slice(start, start + QUERY_ROWS)
+            query = q_ref[here, cols]
+            spans = [(k, v, 0, rows) for k, v in zip(key_refs[:-1], value_refs[:-1])]
+            if start > 0:
+                spans.append((key_refs[-1], value_refs[-1], 0, start))
+            spans.append((key_refs[-1], value_refs[-1], start, start + QUERY_ROWS))
+            scores = [
+                lax.dot_general(query, k[lo:hi, cols], (((1,), (1,)), ((), ())), preferred_element_type=jnp.float32) * scale
+                for k, _, lo, hi in spans
+            ]
+            scores[-1] = jnp.where(causal, scores[-1], -jnp.inf)
+            top = scores[0].max(axis=-1, keepdims=True)
+            for part in scores[1:]:
+                top = jnp.maximum(top, part.max(axis=-1, keepdims=True))
+            weights = [jnp.exp2(part - top) for part in scores]
+            total = weights[0].sum(axis=-1, keepdims=True)
+            for part in weights[1:]:
+                total = total + part.sum(axis=-1, keepdims=True)
+            inverse = 1.0 / total
+            mixed = jnp.zeros((QUERY_ROWS, head_dim), jnp.float32)
+            for part, (_, v, lo, hi) in zip(weights, spans):
+                mixed = mixed + jnp.dot((part * inverse).astype(jnp.bfloat16), v[lo:hi, cols], preferred_element_type=jnp.float32)
+            out_ref[here, cols] = mixed.astype(jnp.bfloat16)
 
 
 def project_block(normed_ref, w_ref):
@@ -90,8 +99,8 @@
 
 def exchange_kernel(head_dim, table_ref, out_rows_ref, resid_ref, gain_ref, wq_ref, wk_ref, wv_ref,
                     arrived_ref, k_ref, v_ref, context_ref, pair_out_ref, cross_out_ref, near_out_ref,
-                    terms_ref, pair_in_ref, near_in_ref, cross_in_ref, base_ref, combined_ref, x_ref, normed_ref,
-                    load_sem, send_sems, recv_sems):
+                    terms_0_ref, terms_1_ref, terms_2_ref, pair_in_ref, near_in_ref, cross_in_ref, base_ref, combined_ref, x_ref, normed_ref,
+                    q_held_ref, k_held_ref, v_held_ref, load_sem, send_sems, recv_sems):
     me = lax.axis_index('ep')
     stage = lax.axis_index('pp')
     seq, model_dim = resid_ref.shape
@@ -109,6 +118,7 @@
     pl.semaphore_wait(barrier, 3)
 
     copies = []
+    terms_refs = (terms_0_ref, terms_1_ref, terms_2_ref)
 
     def send(src_ref, dst_ref, target):
         index = len(copies)
@@ -119,15 +129,19 @@
         copies.append(copy)
         return copy
 
-    def fill(slot, owner, part):
-        fill_gate_terms(table_ref.at[owner], part * half, first_code, terms_ref.at[slot])
-
-    def partial_sums(slot, owner, first, cols, dst_ref, extra_ref=None, resid=None, keep_ref=None):
+    owners = (diagonal, across, partner, me) * HALVES
+    fill_blocks = half // FILL_ROWS
+
+    def fill(job, block):
+        fill_gate_block(table_ref.at[owners[job]], job // 4 * half, first_code, terms_refs[job % GATE_SLOTS], block)
+
+    def partial_sums(job, first, cols, dst_ref=None, extra_ref=None, resid=None, keep_ref=None, ahead=None):
         steps, begin = cols // PART_COLS, first // PART_COLS
+        owner = owners[job]
 
         def body(block_ref, *refs):
             block = block_ref[...].reshape(experts * slot_dev, PART_COLS)
-            sums = jnp.dot(terms_ref[slot], block, preferred_element_type=jnp.float32)
+            sums = jnp.dot(terms_refs[job % GATE_SLOTS][...], block, preferred_element_type=jnp.float32)
             total = sums[:half] + (sums[half:2 * half] + sums[2 * half:])
             at = pl.ds(pl.multiple_of((pl.program_id(0) + begin) * PART_COLS, PART_COLS), PART_COLS)
             if extra_ref is not None:
@@ -138,6 +152,10 @@
                 keep_ref[:, at] = total
             else:
                 refs[-1][...] = total
+            if ahead is not None:
+                per_step = fill_blocks // steps
+                for i in range(per_step):
+                    fill(ahead, pl.program_id(0) * per_step + i)
 
         col_spec = pl.BlockSpec((half, PART_COLS), lambda n: (0, n + begin))
         in_specs = [pl.BlockSpec((experts, slot_dev, PART_COLS), lambda n: (0, owner, n + begin))]
@@ -156,28 +174,28 @@
     def half_rows(part):
         return pl.ds(part * half, half)
 
-    def pair_part(part, first, cols):
+    def pair_part(part, first, cols, ahead=None):
         source = pair_out_ref.at[part]
-        partial_sums(0, diagonal, first, cols, source)
+        partial_sums(4 * part, first, cols, source, ahead=ahead)
         span = col_span(first, cols)
         return send(source.at[span], pair_in_ref.at[span], {'ep': partner})
 
-    def cross_part(part, first, cols, pair):
+    def cross_part(part, first, cols, pair, ahead=None):
         pair.wait_recv()
         source = cross_out_ref.at[part]
-        partial_sums(1, across, first, cols, source, extra_ref=pair_in_ref)
+        partial_sums(4 * part + 1, first, cols, source, extra_ref=pair_in_ref, ahead=ahead)
         for at in range(first, first + cols, SEND_COLS):
             span = col_span(at, SEND_COLS)
             crossed[part].append(send(source.at[span], cross_in_ref.at[part].at[span], {'ep': across}))
 
-    def near_part(part):
+    def near_part(part, ahead=None):
         source = near_out_ref.at[part]
-        partial_sums(0, partner, 0, model_dim, source)
+        partial_sums(4 * part + 2, 0, model_dim, source, ahead=ahead)
         return send(source, near_in_ref, {'ep': partner})
 
-    def base_part(part, near):
+    def base_part(part, near, ahead=None):
         near.wait_recv()
-        partial_sums(1, me, 0, model_dim, None, extra_ref=near_in_ref, resid=resid_ref.at[half_rows(part)], keep_ref=base_ref)
+        partial_sums(4 * part + 3, 0, model_dim, extra_ref=near_in_ref, resid=resid_ref.at[half_rows(part)], keep_ref=base_ref, ahead=ahead)
 
     def finish(part, index):
         if part > 0:
@@ -192,30 +210,27 @@
     moved = [[], []]
     chunks = model_dim // SEND_COLS
     one, rest = SEND_COLS, model_dim - 2 * SEND_COLS
-    fill(0, diagonal, 0)
-    pair_a = pair_part(0, 0, one)
-    fill(1, across, 0)
+
+    @pl.loop(0, fill_blocks)
+    def _(block):
+        fill(0, block)
+
+    pair_a = pair_part(0, 0, one, ahead=1)
     cross_part(0, 0, one, pair_a)
     pair_b = pair_part(0, one, one)
-    pair_c = pair_part(0, 2 * one, rest)
+    pair_c = pair_part(0, 2 * one, rest, ahead=2)
     cross_part(0, one, one, pair_b)
-    cross_part(0, 2 * one, rest, pair_c)
-    fill(0, partner, 0)
-    near = near_part(0)
-    fill(1, me, 0)
-    base_part(0, near)
+    cross_part(0, 2 * one, rest, pair_c, ahead=3)
+    near = near_part(0, ahead=4)
+    base_part(0, near, ahead=5)
     finish(0, 0)
     finish(0, 1)
-    fill(0, diagonal, 1)
-    pair_d = pair_part(1, 0, model_dim)
+    pair_d = pair_part(1, 0, model_dim, ahead=6)
     finish(0, 2)
-    fill(1, across, 1)
-    cross_part(1, 0, model_dim, pair_d)
+    cross_part(1, 0, model_dim, pair_d, ahead=7)
     for index in range(3, chunks):
         finish(0, index)
-    fill(0, partner, 1)
     near = near_part(1)
-    fill(1, me, 1)
 
     for copy in moved[0]:
         copy.wait_recv()
@@ -227,18 +242,29 @@
     group = HEAD_GROUP * head_dim
     groups = k_ref.shape[1] // group
 
+    attend_scratch = (q_held_ref, [k_held_ref], [v_held_ref])
+
     def head_groups(first, count):
         def body(wq_block, wk_block, wv_block, k_block, v_block, context_block):
-            queries, keys, values = [project_block(normed_ref, w) for w in (wq_block, wk_block, wv_block)]
+            attend_heads(*attend_scratch, head_dim, context_block)
+            keys, values = project_block(normed_ref, wk_block), project_block(normed_ref, wv_block)
             k_block[...] = keys
             v_block[...] = values
-            attend_heads(queries, [keys], [values], head_dim, context_block)
+            q_held_ref[...] = project_block(normed_ref, wq_block)
+            k_held_ref[...] = keys
+            v_held_ref[...] = values
 
         out_spec = pl.BlockSpec((half, group), lambda n: (0, n + first))
+        late_spec = pl.BlockSpec((half, group), lambda n: (0, jnp.maximum(n + first - 1, 0)))
         pltpu.emit_pipeline(
-            body, grid=(count,), in_specs=[weight_spec_at(model_dim, group, first)] * 3, out_specs=[out_spec] * 3,
+            body, grid=(count,), in_specs=[weight_spec_at(model_dim, group, first)] * 3, out_specs=[out_spec, out_spec, late_spec],
         )(wq_ref, wk_ref, wv_ref, k_ref, v_ref, context_ref.at[half_rows(0)])
 
+    def last_group(context_block):
+        attend_heads(*attend_scratch, head_dim, context_block)
+
+    for ref in (q_held_ref, k_held_ref, v_held_ref):
+        ref[...] = jnp.zeros_like(ref)
     third = groups // 3
     head_groups(0, third)
     base_part(1, near)
@@ -248,6 +274,8 @@
     for index in range(2, chunks):
         finish(1, index)
     head_groups(2 * third, groups - 2 * third)
+    pltpu.emit_pipeline(last_group, grid=(1,), out_specs=[pl.BlockSpec((half, group), lambda n: (0, groups - 1))])(
+        context_ref.at[half_rows(0)])
     for copy in moved[1]:
         copy.wait_recv()
     already = {id(copy) for copy in moved[0]}
@@ -277,7 +305,7 @@
         in_specs=[VMEM_SPEC, ANY_SPEC, ANY_SPEC, VMEM_SPEC, ANY_SPEC, ANY_SPEC, ANY_SPEC],
         out_specs=[ANY_SPEC] * len(out_shape),
         scratch_shapes=[
-            pltpu.VMEM((2, 3 * half, slots), jnp.bfloat16),
+            *[pltpu.VMEM((3 * half, slots), jnp.bfloat16)] * GATE_SLOTS,
             pltpu.VMEM((half, model_dim), jnp.float32),
             pltpu.VMEM((half, model_dim), jnp.float32),
             pltpu.VMEM((HALVES, half, model_dim), jnp.float32),
@@ -285,6 +313,7 @@
             pltpu.VMEM((half, model_dim), jnp.bfloat16),
             pltpu.VMEM((half, model_dim), jnp.bfloat16),
             pltpu.VMEM((half, model_dim), jnp.bfloat16),
+            *[pltpu.VMEM((half, HEAD_GROUP * head_dim), jnp.bfloat16)] * 3,
             pltpu.SemaphoreType.DMA,
             pltpu.SemaphoreType.DMA((n_copies,)),
             pltpu.SemaphoreType.DMA((n_copies,)),
@@ -295,21 +324,33 @@
     return outs[:4]
 
 
-def second_half_kernel(head_dim, gain_ref, x_ref, wq_ref, wk_ref, wv_ref, k_ref, v_ref, held_ref, context_ref, normed_ref):
+def second_half_kernel(head_dim, gain_ref, x_ref, wq_ref, wk_ref, wv_ref, k_ref, v_ref, held_ref, context_ref,
+                       normed_ref, q_held_ref, k_held_ref, v_held_ref):
     del held_ref
     half, model_dim = x_ref.shape
     normalise(x_ref, gain_ref, normed_ref)
     group = HEAD_GROUP * head_dim
     groups = k_ref.shape[1] // group
+    for ref in (q_held_ref, k_held_ref, v_held_ref):
+        ref[...] = jnp.zeros_like(ref)
+
+    def attend_before(k_block, v_block, context_block):
+        attend_heads(q_held_ref, [k_block, k_held_ref], [v_block, v_held_ref], head_dim, context_block)
 
     def body(wq_block, wk_block, wv_block, k_block, v_block, context_block):
-        queries, keys, values = [project_block(normed_ref, w) for w in (wq_block, wk_block, wv_block)]
-        attend_heads(queries, [k_block[...], keys], [v_block[...], values], head_dim, context_block)
-
-    spec = pl.BlockSpec((half, group), lambda n: (0, n))
+        attend_before(k_block, v_block, context_block)
+        keys, values = project_block(normed_ref, wk_block), project_block(normed_ref, wv_block)
+        q_held_ref[...] = project_block(normed_ref, wq_block)
+        k_held_ref[...] = keys
+        v_held_ref[...] = values
+
+    late_spec = pl.BlockSpec((half, group), lambda n: (0, jnp.maximum(n - 1, 0)))
+    last_spec = pl.BlockSpec((half, group), lambda n: (0, groups - 1))
+    target = context_ref.at[pl.ds(half, half)]
     pltpu.emit_pipeline(
-        body, grid=(groups,), in_specs=[weight_spec_at(model_dim, group, 0)] * 3 + [spec] * 2, out_specs=[spec],
-    )(wq_ref, wk_ref, wv_ref, k_ref, v_ref, context_ref.at[pl.ds(half, half)])
+        body, grid=(groups,), in_specs=[weight_spec_at(model_dim, group, 0)] * 3 + [late_spec] * 2, out_specs=[late_spec],
+    )(wq_ref, wk_ref, wv_ref, k_ref, v_ref, target)
+    pltpu.emit_pipeline(attend_before, grid=(1,), in_specs=[last_spec] * 2, out_specs=[last_spec])(k_ref, v_ref, target)
 
 
 def second_half(arrived, gain, w_query, w_key, w_value, keys, values, context, head_dim):
@@ -323,7 +364,7 @@
         in_specs=[pl.BlockSpec(gain.shape, lambda n: (0, 0)), pl.BlockSpec((half, model_dim), lambda n: (1, 0))] + [ANY_SPEC] * 6,
         out_specs=ANY_SPEC,
         input_output_aliases={7: 0},
-        scratch_shapes=[pltpu.VMEM((half, model_dim), jnp.bfloat16)],
+        scratch_shapes=[pltpu.VMEM((half, model_dim), jnp.bfloat16)] + [pltpu.VMEM((half, HEAD_GROUP * head_dim), jnp.bfloat16)] * 3,
         compiler_params=pltpu.CompilerParams(vmem_limit_bytes=VMEM_LIMIT, dimension_semantics=("arbitrary",)),
         cost_estimate=pl.CostEstimate(flops=6 * half * model_dim * hidden, bytes_accessed=6 * model_dim * hidden, transcendentals=0),
         name="second_half",

time: 549 us -> 572 us (1.042)
  Pallas kernels: 473 us -> 496 us
    pallas_call x1, Pallas kernels: 147 us -> 158 us  [second_half(): pl.pallas_call(functools.partial(second_half_kernel, head_dim), out_shape...]
    pallas_call x1, Pallas kernels: 326 us -> 337 us  [exchange(): pl.pallas_call(functools.partial(exchange_kernel, head_dim), out_shape=ou...]
where the time goes in v2:
time: 572 us; the launch traced here: 571 us
  Pallas kernels  496 us (87%)
  matrix products  62.4 us (11%)
  blocking collectives  10.3 us (2%)
    pallas_call x1, Pallas kernels, exchange(): pl.pallas_call(functools.partial(exchange_kernel, head_dim), out_shape=ou...  337 us
    pallas_call x1, Pallas kernels, second_half(): pl.pallas_call(functools.partial(second_half_kernel, head_dim), out_shape...  158 us
    dot_general x1, matrix products, local_step(): jnp.dot(context, flat_out, preferred_element_type=jnp.float32)  62.4 us

profile of v2, /device:TPU:0, one launch (start us, length us, event | category | flops | bytes accessed | tf_op | source)
XLA Modules:
  0.0 571.2 jit_solution(10541392471860528063)
XLA Ops:
  0.0 0.7 convert_bitcast_fusion
  0.7 0.7 pad_maximum_fusion
  1.5 10.3 %all-gather = f32[64,512]{1,0:T(8,128)S(1)} all-gather(f32[16,512]{1,0:T(8,128)S(1)} %pad_maximum_fusion), channel_id=2, replica_groups=mesh['data'=1,'pp'=2,'ep'=4] {'ep'}, dimensions={0}, use_global_device_ids=true | all-gather | bytes 163840 | tf_op jit(solution)/shard_map/all_gather | solution.py:388
  11.7 1.3 copy.12
  13.0 337.3 %exchange.1 = (bf16[512,4096]{1,0:T(8,128)(2,1)}, bf16[256,12288]{1,0:T(8,128)(2,1)}, bf16[256,12288]{1,0:T(8,128)(2,1)}, bf16[512,12288]{1,0:T(8,128)(2,1)}, f3...) custom-call(f32[4,512,16]{2,1,0:T(8,128)} %bitcast.20, ...), custom_call_target="tpu_custom_call" | custom-call | tf_op jit(solution)/shard_map/exchange/pallas_call | solution.py:302
  350.3 158.5 %second_half.1 = bf16[512,12288]{1,0:T(8,128)(2,1)} custom-call(f32[1,4096]{1,0:T(1,128)} %gain_ref.3, bf16[512,4096]{1,0:T(8,128)(2,1)} %get-tuple-element.9.x_ref, bf16[4096,12288]{1,0:T(8,128)(2,1)} %bitcast.8.wq_ref, bf16[4096,12288]{1,0:T(8,128)(2,1)} %bitcast.9.wk_ref, bf16[4096,12288]{1,0:T(8,128)(2,1)} %bitcast.10.wv_ref, ...), custom_call_target="tpu_custom_call", output_to_operand_aliasing={{}: (7, {})} | custom-call | flops 77309411328 | bytes 301989888 | tf_op jit(solution)/shard_map/second_half/pallas_call | solution.py:360
  508.8 62.4 %fusion = bf16[1,1,1,512,4096]{4,3,2,1,0:T(8,128)(2,1)} fusion(bf16[512,12288]{1,0:T(8,128)(2,1)} %second_half.1, bf16[12288,4096]{1,0:T(8,128)(2,1)} %bitcast.11, bf16[512,4096]{1,0:T(8,128)(2,1)} %get-tuple-element.9.x_ref), kind=kOutput, calls=%fused_computation.2 | convolution fusion | flops 51550093312 | bytes 121634816 | tf_op jit(solution)/shard_map/dot_general | solution.py:395

commit v3 on v2

--- a/solution.py
+++ b/solution.py
@@ -18,7 +18,6 @@
 FILL_ROWS = 32
 FILL_STEP = 16
 GATE_SLOTS = 3
-QUERY_ROWS = 128
 LOG2_E = 1.4426950408889634
 ANY_SPEC = pl.BlockSpec(memory_space=pl.ANY)
 VMEM_SPEC = pl.BlockSpec(memory_space=pltpu.VMEM)
@@ -55,38 +54,45 @@
         normed_ref[first:first + 64] = (x_float * inv_rms * gain_ref[...]).astype(jnp.bfloat16)
 
 
+def head_scores(q_ref, key_refs, head_dim):
+    return [
+        [
+            lax.dot_general(k[:, c:c + head_dim], q_ref[:, c:c + head_dim], (((1,), (1,)), ((), ())), preferred_element_type=jnp.float32)
+            for k in key_refs
+        ]
+        for c in range(0, q_ref.shape[1], head_dim)
+    ]
+
+
+def head_context(all_scores, value_refs, head_dim, out_ref):
+    rows = out_ref.shape[0]
+    scale = head_dim ** -0.5 * LOG2_E
+    k_pos = lax.broadcasted_iota(jnp.int32, (rows, rows), 0)
+    q_pos = lax.broadcasted_iota(jnp.int32, (rows, rows), 1)
+    causal = q_pos >= k_pos
+    probs = []
+    for scores in all_scores:
+        scores = [part * scale for part in scores]
+        scores[-1] = jnp.where(causal, scores[-1], -jnp.inf)
+        top = scores[0].max(axis=0, keepdims=True)
+        for part in scores[1:]:
+            top = jnp.maximum(top, part.max(axis=0, keepdims=True))
+        weights = [jnp.exp2(part - top) for part in scores]
+        total = weights[0].sum(axis=0, keepdims=True)
+        for part in weights[1:]:
+            total = total + part.sum(axis=0, keepdims=True)
+        inverse = 1.0 / total
+        probs.append([(part * inverse).astype(jnp.bfloat16) for part in weights])
+    for h, parts in enumerate(probs):
+        cols = slice(h * head_dim, (h + 1) * head_dim)
+        mixed = jnp.zeros((rows, head_dim), jnp.float32)
+        for part, v in zip(parts, value_refs):
+            mixed = mixed + lax.dot_general(part, v[:, cols], (((0,), (0,)), ((), ())), preferred_element_type=jnp.float32)
+        out_ref[:, cols] = mixed.astype(jnp.bfloat16)
+
+
 def attend_heads(q_ref, key_refs, value_refs, head_dim, out_ref):
-    rows = q_ref.shape[0]
-    scale = head_dim ** -0.5 * LOG2_E
-    q_pos = lax.broadcasted_iota(jnp.int32, (QUERY_ROWS, QUERY_ROWS), 0)
-    k_pos = lax.broadcasted_iota(jnp.int32, (QUERY_ROWS, QUERY_ROWS), 1)
-    causal = q_pos >= k_pos
-    for first in range(0, q_ref.shape[1], head_dim):
-        cols = slice(first, first + head_dim)
-        for start in range(0, rows, QUERY_ROWS):
-            here = slice(start, start + QUERY_ROWS)
-            query = q_ref[here, cols]
-            spans = [(k, v, 0, rows) for k, v in zip(key_refs[:-1], value_refs[:-1])]
-            if start > 0:
-                spans.append((key_refs[-1], value_refs[-1], 0, start))
-            spans.append((key_refs[-1], value_refs[-1], start, start + QUERY_ROWS))
-            scores = [
-                lax.dot_general(query, k[lo:hi, cols], (((1,), (1,)), ((), ())), preferred_element_type=jnp.float32) * scale
-                for k, _, lo, hi in spans
-            ]
-            scores[-1] = jnp.where(causal, scores[-1], -jnp.inf)
-            top = scores[0].max(axis=-1, keepdims=True)
-            for part in scores[1:]:
-                top = jnp.maximum(top, part.max(axis=-1, keepdims=True))
-            weights = [jnp.exp2(part - top) for part in scores]
-            total = weights[0].sum(axis=-1, keepdims=True)
-            for part in weights[1:]:
-                total = total + part.sum(axis=-1, keepdims=True)
-            inverse = 1.0 / total
-            mixed = jnp.zeros((QUERY_ROWS, head_dim), jnp.float32)
-            for part, (_, v, lo, hi) in zip(weights, spans):
-                mixed = mixed + jnp.dot((part * inverse).astype(jnp.bfloat16), v[lo:hi, cols], preferred_element_type=jnp.float32)
-            out_ref[here, cols] = mixed.astype(jnp.bfloat16)
+    head_context(head_scores(q_ref, key_refs, head_dim), value_refs, head_dim, out_ref)
 
 
 def project_block(normed_ref, w_ref):
@@ -174,9 +180,11 @@
     def half_rows(part):
         return pl.ds(part * half, half)
 
-    def pair_part(part, first, cols, ahead=None):
+    def pair_part(part, first, cols, ahead=None, after=None):
         source = pair_out_ref.at[part]
         partial_sums(4 * part, first, cols, source, ahead=ahead)
+        if after is not None:
+            after.wait_recv()
         span = col_span(first, cols)
         return send(source.at[span], pair_in_ref.at[span], {'ep': partner})
 
@@ -193,8 +201,7 @@
         partial_sums(4 * part + 2, 0, model_dim, source, ahead=ahead)
         return send(source, near_in_ref, {'ep': partner})
 
-    def base_part(part, near, ahead=None):
-        near.wait_recv()
+    def base_part(part, ahead=None):
         partial_sums(4 * part + 3, 0, model_dim, extra_ref=near_in_ref, resid=resid_ref.at[half_rows(part)], keep_ref=base_ref, ahead=ahead)
 
     def finish(part, index):
@@ -222,14 +229,17 @@
     cross_part(0, one, one, pair_b)
     cross_part(0, 2 * one, rest, pair_c, ahead=3)
     near = near_part(0, ahead=4)
-    base_part(0, near, ahead=5)
+    middle = model_dim // 2
+    pair_d = pair_part(1, 0, middle, after=near)
+    base_part(0, ahead=5)
     finish(0, 0)
     finish(0, 1)
-    pair_d = pair_part(1, 0, model_dim, ahead=6)
+    pair_e = pair_part(1, middle, middle, ahead=6)
     finish(0, 2)
-    cross_part(1, 0, model_dim, pair_d, ahead=7)
+    cross_part(1, 0, middle, pair_d, ahead=7)
     for index in range(3, chunks):
         finish(0, index)
+    cross_part(1, middle, middle, pair_e)
     near = near_part(1)
 
     for copy in moved[0]:
@@ -242,15 +252,16 @@
     group = HEAD_GROUP * head_dim
     groups = k_ref.shape[1] // group
 
-    attend_scratch = (q_held_ref, [k_held_ref], [v_held_ref])
-
     def head_groups(first, count):
         def body(wq_block, wk_block, wv_block, k_block, v_block, context_block):
-            attend_heads(*attend_scratch, head_dim, context_block)
-            keys, values = project_block(normed_ref, wk_block), project_block(normed_ref, wv_block)
+            scores = head_scores(q_held_ref, [k_held_ref], head_dim)
+            queries = project_block(normed_ref, wq_block)
+            keys = project_block(normed_ref, wk_block)
+            head_context(scores, [v_held_ref], head_dim, context_block)
+            values = project_block(normed_ref, wv_block)
             k_block[...] = keys
             v_block[...] = values
-            q_held_ref[...] = project_block(normed_ref, wq_block)
+            q_held_ref[...] = queries
             k_held_ref[...] = keys
             v_held_ref[...] = values
 
@@ -261,13 +272,14 @@
         )(wq_ref, wk_ref, wv_ref, k_ref, v_ref, context_ref.at[half_rows(0)])
 
     def last_group(context_block):
-        attend_heads(*attend_scratch, head_dim, context_block)
+        attend_heads(q_held_ref, [k_held_ref], [v_held_ref], head_dim, context_block)
 
     for ref in (q_held_ref, k_held_ref, v_held_ref):
         ref[...] = jnp.zeros_like(ref)
     third = groups // 3
     head_groups(0, third)
-    base_part(1, near)
+    near.wait_recv()
+    base_part(1)
     finish(1, 0)
     finish(1, 1)
     head_groups(third, third)
@@ -298,7 +310,7 @@
         staged, staged, staged,
     ]
     chunks = model_dim // SEND_COLS
-    n_copies = 4 + 2 + 2 * HALVES * chunks
+    n_copies = 5 + 2 + 2 * HALVES * chunks
     outs = pl.pallas_call(
         functools.partial(exchange_kernel, head_dim),
         out_shape=out_shape,
@@ -338,9 +350,12 @@
         attend_heads(q_held_ref, [k_block, k_held_ref], [v_block, v_held_ref], head_dim, context_block)
 
     def body(wq_block, wk_block, wv_block, k_block, v_block, context_block):
-        attend_before(k_block, v_block, context_block)
-        keys, values = project_block(normed_ref, wk_block), project_block(normed_ref, wv_block)
-        q_held_ref[...] = project_block(normed_ref, wq_block)
+        scores = head_scores(q_held_ref, [k_block, k_held_ref], head_dim)
+        queries = project_block(normed_ref, wq_block)
+        keys = project_block(normed_ref, wk_block)
+        head_context(scores, [v_block, v_held_ref], head_dim, context_block)
+        values = project_block(normed_ref, wv_block)
+        q_held_ref[...] = queries
         k_held_ref[...] = keys
         v_held_ref[...] = values
 

time: 572 us -> 494 us (0.86)
  Pallas kernels: 496 us -> 417 us
    pallas_call x1, Pallas kernels: 337 us -> 286 us  [exchange(): pl.pallas_call(functools.partial(exchange_kernel, head_dim), out_shape=ou...]
    pallas_call x1, Pallas kernels: 158 us -> 131 us  [second_half(): pl.pallas_call(functools.partial(second_half_kernel, head_dim), out_shape...]
where the time goes in v3:
time: 494 us; the launch traced here: 493 us
  Pallas kernels  417 us (84%)
  matrix products  62.4 us (13%)
  blocking collectives  10.3 us (2%)
    pallas_call x1, Pallas kernels, exchange(): pl.pallas_call(functools.partial(exchange_kernel, head_dim), out_shape=ou...  286 us
    pallas_call x1, Pallas kernels, second_half(): pl.pallas_call(functools.partial(second_half_kernel, head_dim), out_shape...  131 us
    dot_general x1, matrix products, local_step(): jnp.dot(context, flat_out, preferred_element_type=jnp.float32)  62.4 us
    all_gather x1, blocking collectives, local_step(): table = lax.all_gather(own_table, 'ep').transpose(0, 2, 1)  10.3 us

profile of v3, /device:TPU:0, one launch (start us, length us, event | category | flops | bytes accessed | tf_op | source)
XLA Modules:
  0.0 492.9 jit_solution(6048316629850498485)
XLA Ops:
  0.0 0.7 convert_bitcast_fusion
  0.7 0.7 pad_maximum_fusion
  1.5 10.3 %all-gather = f32[64,512]{1,0:T(8,128)S(1)} all-gather(f32[16,512]{1,0:T(8,128)S(1)} %pad_maximum_fusion), channel_id=2, replica_groups=mesh['data'=1,'pp'=2,'ep'=4] {'ep'}, dimensions={0}, use_global_device_ids=true | all-gather | bytes 163840 | tf_op jit(solution)/shard_map/all_gather | solution.py:403
  11.7 1.3 copy.12
  13.0 286.0 %exchange.1 = (bf16[512,4096]{1,0:T(8,128)(2,1)}, bf16[256,12288]{1,0:T(8,128)(2,1)}, bf16[256,12288]{1,0:T(8,128)(2,1)}, bf16[512,12288]{1,0:T(8,128)(2,1)}, f3...) custom-call(f32[4,512,16]{2,1,0:T(8,128)} %bitcast.20, ...), custom_call_target="tpu_custom_call" | custom-call | tf_op jit(solution)/shard_map/exchange/pallas_call | solution.py:314
  299.1 131.4 %second_half.1 = bf16[512,12288]{1,0:T(8,128)(2,1)} custom-call(f32[1,4096]{1,0:T(1,128)} %gain_ref.3, bf16[512,4096]{1,0:T(8,128)(2,1)} %get-tuple-element.9.x_ref, bf16[4096,12288]{1,0:T(8,128)(2,1)} %bitcast.8.wq_ref, bf16[4096,12288]{1,0:T(8,128)(2,1)} %bitcast.9.wk_ref, bf16[4096,12288]{1,0:T(8,128)(2,1)} %bitcast.10.wv_ref, ...), custom_call_target="tpu_custom_call", output_to_operand_aliasing={{}: (7, {})} | custom-call | flops 77309411328 | bytes 301989888 | tf_op jit(solution)/shard_map/second_half/pallas_call | solution.py:375
  430.5 62.4 %fusion = bf16[1,1,1,512,4096]{4,3,2,1,0:T(8,128)(2,1)} fusion(bf16[512,12288]{1,0:T(8,128)(2,1)} %second_half.1, bf16[12288,4096]{1,0:T(8,128)(2,1)} %bitcast.11, bf16[512,4096]{1,0:T(8,128)(2,1)} %get-tuple-element.9.x_ref), kind=kOutput, calls=%fused_computation.2 | convolution fusion | flops 51550093312 | bytes 121634816 | tf_op jit(solution)/shard_map/dot_general | solution.py:410

commit v4 on v3

--- a/solution.py
+++ b/solution.py
@@ -12,8 +12,7 @@
 VMEM_LIMIT = 62 * 2**20
 PART_COLS = 512
 SEND_COLS = 1024
-HEAD_GROUP = 2
-WEIGHT_BUFFERS = 3
+HEAD_GROUP = 4
 HALVES = 2
 FILL_ROWS = 32
 FILL_STEP = 16
@@ -99,13 +98,31 @@
     return jnp.dot(normed_ref[...], w_ref[...], preferred_element_type=jnp.float32).astype(jnp.bfloat16)
 
 
-def weight_spec_at(model_dim, cols, first):
-    return pl.BlockSpec((model_dim, cols), lambda n: (0, n + first), pipeline_mode=pl.Buffered(WEIGHT_BUFFERS))
+def weight_spec_at(model_dim, cols, first, buffers):
+    return pl.BlockSpec((model_dim, cols), lambda n: (0, n + first), pipeline_mode=pl.Buffered(buffers))
+
+
+class Transfer:
+    def __init__(self, make_refs, target, send_sems, recv_sems, index):
+        self.parts = (make_refs, target, send_sems, recv_sems, index)
+
+    def describe(self):
+        make_refs, target, send_sems, recv_sems, index = self.parts
+        src_ref, dst_ref = make_refs()
+        return pltpu.make_async_remote_copy(
+            src_ref=src_ref, dst_ref=dst_ref, send_sem=send_sems.at[index], recv_sem=recv_sems.at[index],
+            device_id=target, device_id_type=pl.DeviceIdType.MESH)
+
+    def wait_send(self):
+        self.describe().wait_send()
+
+    def wait_recv(self):
+        self.describe().wait_recv()
 
 
 def exchange_kernel(head_dim, table_ref, out_rows_ref, resid_ref, gain_ref, wq_ref, wk_ref, wv_ref,
                     arrived_ref, k_ref, v_ref, context_ref, pair_out_ref, cross_out_ref, near_out_ref,
-                    terms_0_ref, terms_1_ref, terms_2_ref, pair_in_ref, near_in_ref, cross_in_ref, base_ref, combined_ref, x_ref, normed_ref,
+                    pair_in_ref, near_in_ref, cross_in_ref, base_ref, combined_ref, x_ref, normed_ref,
                     q_held_ref, k_held_ref, v_held_ref, load_sem, send_sems, recv_sems):
     me = lax.axis_index('ep')
     stage = lax.axis_index('pp')
@@ -124,16 +141,13 @@
     pl.semaphore_wait(barrier, 3)
 
     copies = []
-    terms_refs = (terms_0_ref, terms_1_ref, terms_2_ref)
-
-    def send(src_ref, dst_ref, target):
-        index = len(copies)
-        copy = pltpu.make_async_remote_copy(
-            src_ref=src_ref, dst_ref=dst_ref, send_sem=send_sems.at[index], recv_sem=recv_sems.at[index],
-            device_id=target, device_id_type=pl.DeviceIdType.MESH)
-        copy.start()
-        copies.append(copy)
-        return copy
+    terms_refs = []
+
+    def send(make_refs, target):
+        transfer = Transfer(make_refs, target, send_sems, recv_sems, len(copies))
+        transfer.describe().start()
+        copies.append(transfer)
+        return transfer
 
     owners = (diagonal, across, partner, me) * HALVES
     fill_blocks = half // FILL_ROWS
@@ -186,20 +200,23 @@
         if after is not None:
             after.wait_recv()
         span = col_span(first, cols)
-        return send(source.at[span], pair_in_ref.at[span], {'ep': partner})
-
-    def cross_part(part, first, cols, pair, ahead=None):
-        pair.wait_recv()
+        return send(lambda: (pair_out_ref.at[part].at[span], pair_in_ref.at[span]), {'ep': partner})
+
+    def cross_part(part, first, cols, pair=None, ahead=None):
+        if pair is not None:
+            pair.wait_recv()
         source = cross_out_ref.at[part]
         partial_sums(4 * part + 1, first, cols, source, extra_ref=pair_in_ref, ahead=ahead)
         for at in range(first, first + cols, SEND_COLS):
             span = col_span(at, SEND_COLS)
-            crossed[part].append(send(source.at[span], cross_in_ref.at[part].at[span], {'ep': across}))
-
-    def near_part(part, ahead=None):
+            crossed[part].append(send(lambda span=span: (cross_out_ref.at[part].at[span], cross_in_ref.at[part].at[span]), {'ep': across}))
+
+    def near_part(part, ahead=None, after=None):
         source = near_out_ref.at[part]
         partial_sums(4 * part + 2, 0, model_dim, source, ahead=ahead)
-        return send(source, near_in_ref, {'ep': partner})
+        if after is not None:
+            after.wait_recv()
+        return send(lambda: (near_out_ref.at[part], near_in_ref), {'ep': partner})
 
     def base_part(part, ahead=None):
         partial_sums(4 * part + 3, 0, model_dim, extra_ref=near_in_ref, resid=resid_ref.at[half_rows(part)], keep_ref=base_ref, ahead=ahead)
@@ -210,38 +227,44 @@
         crossed[part][index].wait_recv()
         span = col_span(index * SEND_COLS, SEND_COLS)
         combined_ref[span] = (base_ref[span] + cross_in_ref[(part,) + span]).astype(jnp.bfloat16)
-        target = arrived_ref.at[half_rows(part), pl.ds(index * SEND_COLS, SEND_COLS)]
-        moved[part].append(send(combined_ref.at[span], target, {'pp': next_stage}))
+        target = (half_rows(part), pl.ds(index * SEND_COLS, SEND_COLS))
+        moved[part].append(send(lambda: (combined_ref.at[span], arrived_ref.at[target]), {'pp': next_stage}))
 
     crossed = [[], []]
     moved = [[], []]
     chunks = model_dim // SEND_COLS
     one, rest = SEND_COLS, model_dim - 2 * SEND_COLS
-
-    @pl.loop(0, fill_blocks)
-    def _(block):
-        fill(0, block)
-
-    pair_a = pair_part(0, 0, one, ahead=1)
-    cross_part(0, 0, one, pair_a)
-    pair_b = pair_part(0, one, one)
-    pair_c = pair_part(0, 2 * one, rest, ahead=2)
-    cross_part(0, one, one, pair_b)
-    cross_part(0, 2 * one, rest, pair_c, ahead=3)
-    near = near_part(0, ahead=4)
     middle = model_dim // 2
-    pair_d = pair_part(1, 0, middle, after=near)
-    base_part(0, ahead=5)
-    finish(0, 0)
-    finish(0, 1)
-    pair_e = pair_part(1, middle, middle, ahead=6)
-    finish(0, 2)
-    cross_part(1, 0, middle, pair_d, ahead=7)
-    for index in range(3, chunks):
-        finish(0, index)
-    cross_part(1, middle, middle, pair_e)
-    near = near_part(1)
-
+
+    def sum_phase(*terms):
+        terms_refs.extend(terms)
+
+        @pl.loop(0, fill_blocks)
+        def _(block):
+            fill(0, block)
+
+        pair_a = pair_part(0, 0, one, ahead=1)
+        cross_part(0, 0, one, pair_a)
+        pair_b = pair_part(0, one, one)
+        pair_c = pair_part(0, 2 * one, rest, ahead=2)
+        cross_part(0, one, one, pair_b)
+        cross_part(0, 2 * one, rest, pair_c, ahead=3)
+        near = near_part(0, ahead=4)
+        pair_d = pair_part(1, 0, middle, after=near)
+        base_part(0, ahead=5)
+        finish(0, 0)
+        finish(0, 1)
+        pair_e = pair_part(1, middle, middle, ahead=6)
+        finish(0, 2)
+        cross_part(1, 0, middle, pair_d, ahead=7)
+        for index in range(3, chunks):
+            finish(0, index)
+        near = near_part(1, after=pair_e)
+        cross_part(1, middle, middle)
+        near.wait_recv()
+        base_part(1)
+
+    pl.run_scoped(sum_phase, *[pltpu.VMEM((3 * half, experts * slot_dev), jnp.bfloat16)] * GATE_SLOTS)
     for copy in moved[0]:
         copy.wait_recv()
     load = pltpu.make_async_copy(arrived_ref.at[half_rows(0)], x_ref, load_sem)
@@ -268,7 +291,7 @@
         out_spec = pl.BlockSpec((half, group), lambda n: (0, n + first))
         late_spec = pl.BlockSpec((half, group), lambda n: (0, jnp.maximum(n + first - 1, 0)))
         pltpu.emit_pipeline(
-            body, grid=(count,), in_specs=[weight_spec_at(model_dim, group, first)] * 3, out_specs=[out_spec, out_spec, late_spec],
+            body, grid=(count,), in_specs=[weight_spec_at(model_dim, group, first, 2)] * 3, out_specs=[out_spec, out_spec, late_spec],
         )(wq_ref, wk_ref, wv_ref, k_ref, v_ref, context_ref.at[half_rows(0)])
 
     def last_group(context_block):
@@ -278,13 +301,10 @@
         ref[...] = jnp.zeros_like(ref)
     third = groups // 3
     head_groups(0, third)
-    near.wait_recv()
-    base_part(1)
-    finish(1, 0)
-    finish(1, 1)
+    for index in range(chunks - 1):
+        finish(1, index)
     head_groups(third, third)
-    for index in range(2, chunks):
-        finish(1, index)
+    finish(1, chunks - 1)
     head_groups(2 * third, groups - 2 * third)
     pltpu.emit_pipeline(last_group, grid=(1,), out_specs=[pl.BlockSpec((half, group), lambda n: (0, groups - 1))])(
         context_ref.at[half_rows(0)])
@@ -300,7 +320,6 @@
     seq, model_dim = own_resid.shape
     hidden = w_query.shape[1]
     half = seq // HALVES
-    slots = own_out.shape[0] * own_out.shape[1] // table.shape[0]
     staged = jax.ShapeDtypeStruct((HALVES, half, model_dim), jnp.float32)
     out_shape = [
         jax.ShapeDtypeStruct((seq, model_dim), jnp.bfloat16),
@@ -317,7 +336,6 @@
         in_specs=[VMEM_SPEC, ANY_SPEC, ANY_SPEC, VMEM_SPEC, ANY_SPEC, ANY_SPEC, ANY_SPEC],
         out_specs=[ANY_SPEC] * len(out_shape),
         scratch_shapes=[
-            *[pltpu.VMEM((3 * half, slots), jnp.bfloat16)] * GATE_SLOTS,
             pltpu.VMEM((half, model_dim), jnp.float32),
             pltpu.VMEM((half, model_dim), jnp.float32),
             pltpu.VMEM((HALVES, half, model_dim), jnp.float32),
@@ -363,7 +381,7 @@
     last_spec = pl.BlockSpec((half, group), lambda n: (0, groups - 1))
     target = context_ref.at[pl.ds(half, half)]
     pltpu.emit_pipeline(
-        body, grid=(groups,), in_specs=[weight_spec_at(model_dim, group, 0)] * 3 + [late_spec] * 2, out_specs=[late_spec],
+        body, grid=(groups,), in_specs=[weight_spec_at(model_dim, group, 0, 3)] * 3 + [late_spec] * 2, out_specs=[late_spec],
     )(wq_ref, wk_ref, wv_ref, k_ref, v_ref, target)
     pltpu.emit_pipeline(attend_before, grid=(1,), in_specs=[last_spec] * 2, out_specs=[last_spec])(k_ref, v_ref, target)
 

time: 494 us -> 493 us (level)
    pallas_call x1, Pallas kernels: 131 us -> 124 us  [second_half(): pl.pallas_call(functools.partial(second_half_kernel, head_dim), out_shape...]
    pallas_call x1, Pallas kernels: 286 us -> 293 us  [exchange(): pl.pallas_call(functools.partial(exchange_kernel, head_dim), out_shape=ou...]
where the time goes in v4:
time: 493 us; the launch traced here: 492 us
  Pallas kernels  417 us (85%)
  matrix products  62.4 us (13%)
  blocking collectives  10.3 us (2%)
    pallas_call x1, Pallas kernels, exchange(): pl.pallas_call(functools.partial(exchange_kernel, head_dim), out_shape=ou...  293 us
    pallas_call x1, Pallas kernels, second_half(): pl.pallas_call(functools.partial(second_half_kernel, head_dim), out_shape...  124 us
    dot_general x1, matrix products, local_step(): jnp.dot(context, flat_out, preferred_element_type=jnp.float32)  62.4 us
    all_gather x1, blocking collectives, local_step(): table = lax.all_gather(own_table, 'ep').transpose(0, 2, 1)  10.3 us

profile of v4, /device:TPU:0, one launch (start us, length us, event | category | flops | bytes accessed | tf_op | source)
XLA Modules:
  0.0 492.0 jit_solution(12809764551379075202)
XLA Ops:
  0.0 0.7 convert_bitcast_fusion
  0.7 0.7 pad_maximum_fusion
  1.5 10.3 %all-gather = f32[64,512]{1,0:T(8,128)S(1)} all-gather(f32[16,512]{1,0:T(8,128)S(1)} %pad_maximum_fusion), channel_id=2, replica_groups=mesh['data'=1,'pp'=2,'ep'=4] {'ep'}, dimensions={0}, use_global_device_ids=true | all-gather | bytes 163840 | tf_op jit(solution)/shard_map/all_gather | solution.py:421
  11.7 1.3 copy.12
  13.0 292.9 %exchange.1 = (bf16[512,4096]{1,0:T(8,128)(2,1)}, bf16[256,12288]{1,0:T(8,128)(2,1)}, bf16[256,12288]{1,0:T(8,128)(2,1)}, bf16[512,12288]{1,0:T(8,128)(2,1)}, f3...) custom-call(f32[4,512,16]{2,1,0:T(8,128)} %bitcast.20, ...), custom_call_target="tpu_custom_call" | custom-call | tf_op jit(solution)/shard_map/exchange/pallas_call | solution.py:333
  306.0 123.6 %second_half.1 = bf16[512,12288]{1,0:T(8,128)(2,1)} custom-call(f32[1,4096]{1,0:T(1,128)} %gain_ref.3, bf16[512,4096]{1,0:T(8,128)(2,1)} %get-tuple-element.9.x_ref, bf16[4096,12288]{1,0:T(8,128)(2,1)} %bitcast.8.wq_ref, bf16[4096,12288]{1,0:T(8,128)(2,1)} %bitcast.9.wk_ref, bf16[4096,12288]{1,0:T(8,128)(2,1)} %bitcast.10.wv_ref, ...), custom_call_target="tpu_custom_call", output_to_operand_aliasing={{}: (7, {})} | custom-call | flops 77309411328 | bytes 301989888 | tf_op jit(solution)/shard_map/second_half/pallas_call | solution.py:393
  429.6 62.4 %fusion = bf16[1,1,1,512,4096]{4,3,2,1,0:T(8,128)(2,1)} fusion(bf16[512,12288]{1,0:T(8,128)(2,1)} %second_half.1, bf16[12288,4096]{1,0:T(8,128)(2,1)} %bitcast.11, bf16[512,4096]{1,0:T(8,128)(2,1)} %get-tuple-element.9.x_ref), kind=kOutput, calls=%fused_computation.2 | convolution fusion | flops 51550093312 | bytes 121634816 | tf_op jit(solution)/shard_map/dot_general | solution.py:428

commit v5 on v3

--- a/solution.py
+++ b/solution.py
@@ -13,6 +13,7 @@
 PART_COLS = 512
 SEND_COLS = 1024
 HEAD_GROUP = 2
+LAST_GROUP = 4
 WEIGHT_BUFFERS = 3
 HALVES = 2
 FILL_ROWS = 32
@@ -103,9 +104,9 @@
     return pl.BlockSpec((model_dim, cols), lambda n: (0, n + first), pipeline_mode=pl.Buffered(WEIGHT_BUFFERS))
 
 
-def exchange_kernel(head_dim, table_ref, out_rows_ref, resid_ref, gain_ref, wq_ref, wk_ref, wv_ref,
+def exchange_kernel(head_dim, own_table_ref, out_rows_ref, resid_ref, gain_ref, wq_ref, wk_ref, wv_ref,
                     arrived_ref, k_ref, v_ref, context_ref, pair_out_ref, cross_out_ref, near_out_ref,
-                    terms_0_ref, terms_1_ref, terms_2_ref, pair_in_ref, near_in_ref, cross_in_ref, base_ref, combined_ref, x_ref, normed_ref,
+                    terms_0_ref, terms_1_ref, terms_2_ref, tables_ref, table_ref, pair_in_ref, near_in_ref, cross_in_ref, base_ref, combined_ref, x_ref, normed_ref,
                     q_held_ref, k_held_ref, v_held_ref, load_sem, send_sems, recv_sems):
     me = lax.axis_index('ep')
     stage = lax.axis_index('pp')
@@ -120,8 +121,9 @@
     barrier = pltpu.get_barrier_semaphore()
     pl.semaphore_signal(barrier, inc=1, device_id={'ep': partner}, device_id_type=pl.DeviceIdType.MESH)
     pl.semaphore_signal(barrier, inc=1, device_id={'ep': across}, device_id_type=pl.DeviceIdType.MESH)
+    pl.semaphore_signal(barrier, inc=1, device_id={'ep': diagonal}, device_id_type=pl.DeviceIdType.MESH)
     pl.semaphore_signal(barrier, inc=1, device_id={'pp': next_stage}, device_id_type=pl.DeviceIdType.MESH)
-    pl.semaphore_wait(barrier, 3)
+    pl.semaphore_wait(barrier, 4)
 
     copies = []
     terms_refs = (terms_0_ref, terms_1_ref, terms_2_ref)
@@ -134,6 +136,13 @@
         copy.start()
         copies.append(copy)
         return copy
+
+    tables_ref[me] = own_table_ref[...]
+    shared = [send(own_table_ref, tables_ref.at[me], {'ep': peer}) for peer in (partner, across, diagonal)]
+    for copy in shared:
+        copy.wait_recv()
+    for owner in range(tables_ref.shape[0]):
+        table_ref[owner] = tables_ref[owner].T
 
     owners = (diagonal, across, partner, me) * HALVES
     fill_blocks = half // FILL_ROWS
@@ -296,11 +305,11 @@
             copy.wait_send()
 
 
-def exchange(table, own_out, own_resid, gain, w_query, w_key, w_value, head_dim):
+def exchange(own_table, ep_size, own_out, own_resid, gain, w_query, w_key, w_value, head_dim):
     seq, model_dim = own_resid.shape
     hidden = w_query.shape[1]
     half = seq // HALVES
-    slots = own_out.shape[0] * own_out.shape[1] // table.shape[0]
+    slots = own_out.shape[0] * own_out.shape[1] // ep_size
     staged = jax.ShapeDtypeStruct((HALVES, half, model_dim), jnp.float32)
     out_shape = [
         jax.ShapeDtypeStruct((seq, model_dim), jnp.bfloat16),
@@ -310,7 +319,7 @@
         staged, staged, staged,
     ]
     chunks = model_dim // SEND_COLS
-    n_copies = 5 + 2 + 2 * HALVES * chunks
+    n_copies = 3 + 5 + 2 + 2 * HALVES * chunks
     outs = pl.pallas_call(
         functools.partial(exchange_kernel, head_dim),
         out_shape=out_shape,
@@ -318,6 +327,8 @@
         out_specs=[ANY_SPEC] * len(out_shape),
         scratch_shapes=[
             *[pltpu.VMEM((3 * half, slots), jnp.bfloat16)] * GATE_SLOTS,
+            pltpu.VMEM((ep_size,) + own_table.shape, jnp.float32),
+            pltpu.VMEM((ep_size,) + own_table.shape[::-1], jnp.float32),
             pltpu.VMEM((half, model_dim), jnp.float32),
             pltpu.VMEM((half, model_dim), jnp.float32),
             pltpu.VMEM((HALVES, half, model_dim), jnp.float32),
@@ -332,7 +343,7 @@
         ],
         compiler_params=pltpu.CompilerParams(vmem_limit_bytes=VMEM_LIMIT, collective_id=0, has_side_effects=True),
         name="exchange",
-    )(table, own_out, own_resid, gain, w_query, w_key, w_value)
+    )(own_table, own_out, own_resid, gain, w_query, w_key, w_value)
     return outs[:4]
 
 
@@ -341,7 +352,7 @@
     del held_ref
     half, model_dim = x_ref.shape
     normalise(x_ref, gain_ref, normed_ref)
-    group = HEAD_GROUP * head_dim
+    group = LAST_GROUP * head_dim
     groups = k_ref.shape[1] // group
     for ref in (q_held_ref, k_held_ref, v_held_ref):
         ref[...] = jnp.zeros_like(ref)
@@ -379,7 +390,7 @@
         in_specs=[pl.BlockSpec(gain.shape, lambda n: (0, 0)), pl.BlockSpec((half, model_dim), lambda n: (1, 0))] + [ANY_SPEC] * 6,
         out_specs=ANY_SPEC,
         input_output_aliases={7: 0},
-        scratch_shapes=[pltpu.VMEM((half, model_dim), jnp.bfloat16)] + [pltpu.VMEM((half, HEAD_GROUP * head_dim), jnp.bfloat16)] * 3,
+        scratch_shapes=[pltpu.VMEM((half, model_dim), jnp.bfloat16)] + [pltpu.VMEM((half, LAST_GROUP * head_dim), jnp.bfloat16)] * 3,
         compiler_params=pltpu.CompilerParams(vmem_limit_bytes=VMEM_LIMIT, dimension_semantics=("arbitrary",)),
         cost_estimate=pl.CostEstimate(flops=6 * half * model_dim * hidden, bytes_accessed=6 * model_dim * hidden, transcendentals=0),
         name="second_half",
@@ -400,11 +411,10 @@
         ids, slots, own_gates = expert_ids[0, 0, 0], slot_ids[0, 0, 0], gates[0, 0, 0]
         code = jnp.where(slots >= 0, ids * slot_dev + (slots - me * slot_dev), -1).astype(jnp.float32)
         own_table = jnp.concatenate([code.T, own_gates.T], axis=0)
-        table = lax.all_gather(own_table, 'ep').transpose(0, 2, 1)
         gain = norm_scale.reshape(1, model_dim)
         head_count, head_dim = w_out.shape[1], w_out.shape[2]
         weights = (w_query[0], w_key[0], w_value[0])
-        arrived, keys, values, context = exchange(table, own_out, own_resid, gain, *weights, head_dim)
+        arrived, keys, values, context = exchange(own_table, ep_size, own_out, own_resid, gain, *weights, head_dim)
         context = second_half(arrived, gain, *weights, keys, values, context, head_dim)
         flat_out = w_out[0].reshape(head_count * head_dim, model_dim)
         proj = jnp.dot(context, flat_out, preferred_element_type=jnp.float32).astype(jnp.bfloat16)

time: 494 us -> 481 us (0.974)
  blocking collectives: 10.3 us -> 0 us
    all_gather x1 -> x0, blocking collectives: 10.3 us -> none  [local_step(): table = lax.all_gather(own_table, 'ep').transpose(0, 2, 1)]
    pallas_call x1, Pallas kernels: 131 us -> 124 us  [second_half(): pl.pallas_call(functools.partial(second_half_kernel, head_dim), out_shape...]
    pallas_call x1, Pallas kernels: 286 us -> 292 us  [exchange(): pl.pallas_call(functools.partial(exchange_kernel, head_dim), out_shape=ou...]
where the time goes in v5:
time: 481 us; the launch traced here: 480 us
  Pallas kernels  416 us (86%)
  matrix products  62.4 us (13%)
    pallas_call x1, Pallas kernels, exchange(): pl.pallas_call(functools.partial(exchange_kernel, head_dim), out_shape=ou...  292 us
    pallas_call x1, Pallas kernels, second_half(): pl.pallas_call(functools.partial(second_half_kernel, head_dim), out_shape...  124 us
    dot_general x1, matrix products, local_step(): jnp.dot(context, flat_out, preferred_element_type=jnp.float32)  62.4 us

profile of v5, /device:TPU:0, one launch (start us, length us, event | category | flops | bytes accessed | tf_op | source)
XLA Modules:
  0.0 480.4 jit_solution(2410159925206474780)
XLA Ops:
  0.0 0.7 convert_bitcast_fusion
  0.7 1.3 pad_maximum_fusion.own_table_ref
  2.1 292.3 %exchange.1 = (bf16[512,4096]{1,0:T(8,128)(2,1)}, bf16[256,12288]{1,0:T(8,128)(2,1)}, bf16[256,12288]{1,0:T(8,128)(2,1)}, bf16[512,12288]{1,0:T(8,128)(2,1)}, f3...) custom-call(f32[16,512]{1,0:T(8,128)} %pad_maximum_fusion.own_table_ref, ...), custom_call_target="tpu_custom_call" | custom-call | tf_op jit(solution)/shard_map/exchange/pallas_call | solution.py:323
  294.4 123.6 %second_half.1 = bf16[512,12288]{1,0:T(8,128)(2,1)} custom-call(f32[1,4096]{1,0:T(1,128)} %gain_ref.3, bf16[512,4096]{1,0:T(8,128)(2,1)} %get-tuple-element.9.x_ref, bf16[4096,12288]{1,0:T(8,128)(2,1)} %bitcast.6.wq_ref, bf16[4096,12288]{1,0:T(8,128)(2,1)} %bitcast.7.wk_ref, bf16[4096,12288]{1,0:T(8,128)(2,1)} %bitcast.8.wv_ref, ...), custom_call_target="tpu_custom_call", output_to_operand_aliasing={{}: (7, {})} | custom-call | flops 77309411328 | bytes 301989888 | tf_op jit(solution)/shard_map/second_half/pallas_call | solution.py:386
  418.0 62.4 %fusion = bf16[1,1,1,512,4096]{4,3,2,1,0:T(8,128)(2,1)} fusion(bf16[512,12288]{1,0:T(8,128)(2,1)} %second_half.1, bf16[12288,4096]{1,0:T(8,128)(2,1)} %bitcast.9, bf16[512,4096]{1,0:T(8,128)(2,1)} %get-tuple-element.9.x_ref), kind=kOutput, calls=%fused_computation.2 | convolution fusion | flops 51550093312 | bytes 121634816 | tf_op jit(solution)/shard_map/dot_general | solution.py:420
